TPU v7x, 256 devices: a whole 4x4x8 slice. The times are simulated.
256 devices in a mesh: dp: 4 (over z_hi), expert: 8 (over z_lo, x), tensor: 8 (over y, core).
Axes of the slice: x: 4, y: 4, z: 8 (z_hi: 4, z_lo: 2; z = z_hi * 2 + z_lo), core: 2. Of those that a mesh axis runs over, the one named last changes fastest.
Arguments:
- tokens: bfloat16 [2048, 4096], P(('dp', 'expert', 'tensor')), may hold values from -6 to 6
- out_grad: bfloat16 [2048, 4096], P(('dp', 'expert', 'tensor')), may hold values from -4 to 4
- route_probs: float32 [2048, 2], P(('dp', 'expert')), may hold values from 0.2 to 1
- expert_ids: int32 [2048, 2], P(('dp', 'expert')), may hold values from 0 to 7, as said below
- slot_index: int32 [2048, 2], P(('dp', 'expert')), may hold values from 0 to 20, as said below
- w_gate: bfloat16 [8, 4096, 7168], P('expert', 'dp', 'tensor'), may hold values from -0.09375 to 0.09375
- w_up: bfloat16 [8, 4096, 7168], P('expert', 'dp', 'tensor'), may hold values from -0.09375 to 0.09375
- w_down: bfloat16 [8, 7168, 4096], P('expert', 'tensor', 'dp'), may hold values from -0.0625 to 0.0625
Outputs:
- token_grad: bfloat16 [2048, 4096], P(('dp', 'expert', 'tensor'))
- grad_gate: bfloat16 [8, 4096, 7168], P('expert', 'dp', 'tensor')
- grad_up: bfloat16 [8, 4096, 7168], P('expert', 'dp', 'tensor')
- grad_down: bfloat16 [8, 7168, 4096], P('expert', 'tensor', 'dp')
Inputs may be any that keep to these rules, and one draw needn't show every extreme that they name: `expert_ids`: the 2 entries of a token are different experts. slot_index[t, k] counts the earlier routes to expert_ids[t, k] within the token's routing block of 64 rows, in order of tokens and then of routes; the value 20 marks a route past the capacity, which is dropped (a count of 20 or more is given as 20). In every draw some expert is filled to 20 slots in every block.
All inputs are finite; a program needn't handle non-finite values.
Results may differ from a plain program's by a relative error of at most 0.011.
Values may be sent and summed in bfloat16 or wider, within the bound.
A program may use at most 128 MiB of HBM per device.

v0:
```python
import jax
import jax.numpy as jnp
from jax import lax
from jax.sharding import PartitionSpec as P

EXPERTS = 8
TOP = 2


def in_one_piece(arrays, axis, dim, along):
    ends, at = ([], 0)
    for a in arrays[:-1]:
        at += a.shape[along]
        ends.append(at)
    both = jnp.concatenate(arrays, axis=along)
    return tuple(jnp.split(lax.all_gather(both, axis, axis=dim, tiled=True), ends, axis=along))


def in_blocks(shard, dim, length):
    before, after = (shard.shape[:dim], shard.shape[dim + 1 :])
    return jnp.moveaxis(shard.reshape(*before, length, -1, *after), dim, 0)


def laid_out(pieces, dim):
    pieces = jnp.moveaxis(pieces, 0, dim)
    dims = pieces.shape
    return pieces.reshape(*dims[:dim], dims[dim] * dims[dim + 1], *dims[dim + 2 :])


def exchange_both(shard, axis, axes, splits, concats):
    sizes = [lax.axis_size(a) for a in axes]
    pieces = in_blocks(shard, splits[0], sizes[0])
    pieces = jnp.moveaxis(in_blocks(pieces, splits[1] + 1, sizes[1]), 0, 1)
    inside = pieces.shape[2:]
    pieces = pieces.reshape(-1, *inside)
    pieces = lax.all_to_all(pieces, axis, split_axis=0, concat_axis=0, tiled=True)
    pieces = laid_out(pieces.reshape(*sizes, *inside), concats[0] + 1)
    return laid_out(pieces, concats[1])


def sum_at_owner(shard, axis, dim):
    pieces = in_blocks(shard, dim, lax.axis_size(axis))
    arrived = lax.all_to_all(pieces, axis, split_axis=0, concat_axis=0, tiled=True)
    return arrived.astype(jnp.float32).sum(axis=0)


def sum_at_owner_2(shard, axis, dim):
    pieces = in_blocks(shard, dim, lax.axis_size(axis))
    arrived = lax.all_to_all(pieces, axis, split_axis=0, concat_axis=0, tiled=True)
    return arrived.sum(axis=0)


def route_tables(expert_ids, slot_index, capacity):
    target = slot_index * EXPERTS + expert_ids
    target = jnp.where(slot_index < capacity, target, -1)
    places = jnp.arange(capacity * EXPERTS, dtype=jnp.int32)
    return [(places[:, None] == target[None, :, k]).astype(jnp.bfloat16) for k in range(TOP)]


def swiglu_back(pre_gate, pre_up, grad_hidden):
    sigmoid_gate = jax.nn.sigmoid(pre_gate)
    silu_gate = pre_gate * sigmoid_gate
    hidden = (silu_gate * pre_up).astype(jnp.bfloat16)
    up_delta = (grad_hidden * silu_gate).astype(jnp.bfloat16)
    gate_delta = (
        grad_hidden * pre_up * sigmoid_gate * (1.0 + pre_gate * (1.0 - sigmoid_gate))
    ).astype(jnp.bfloat16)
    return (hidden, gate_delta, up_delta)


def shards(tokens, out_grad, route_probs, expert_ids, slot_index, w_gate, w_up, w_down):
    block_x, block_dy = in_one_piece((tokens, out_grad), "tensor", 0, 1)
    block_rows = block_x.shape[0]
    model_width = block_x.shape[1]
    local_rows = tokens.shape[0]
    capacity = 5 * block_rows * TOP // (4 * EXPERTS)
    tables = route_tables(expert_ids, slot_index, capacity)
    table_sum = tables[0] + tables[1]
    x_buf = jnp.dot(table_sum, block_x, preferred_element_type=jnp.float32).astype(jnp.bfloat16)
    grad_buf = jnp.zeros((capacity * EXPERTS, model_width), jnp.float32)
    for k in range(TOP):
        scaled = (route_probs[:, k : k + 1] * block_dy.astype(jnp.float32)).astype(jnp.bfloat16)
        grad_buf = grad_buf + jnp.dot(tables[k], scaled, preferred_element_type=jnp.float32)
    grad_buf = grad_buf.astype(jnp.bfloat16)
    recv_x, recv_grad = (
        exchange_both(
            x_buf.reshape(capacity, EXPERTS, model_width),
            ("dp", "expert"),
            ("dp", "expert"),
            (2, 1),
            (0, 1),
        ),
        exchange_both(
            grad_buf.reshape(capacity, EXPERTS, model_width),
            ("dp", "expert"),
            ("dp", "expert"),
            (2, 1),
            (0, 1),
        ),
    )
    local_experts = w_gate.shape[0]
    sources = EXPERTS // local_experts
    rows_all = recv_x.shape[0]
    slice_width = recv_x.shape[2]
    token_rows = recv_x.reshape(rows_all, sources, local_experts, slice_width)
    grad_rows = recv_grad.reshape(rows_all, sources, local_experts, slice_width)
    pre_gate = jnp.einsum("cnld,ldf->cnlf", token_rows, w_gate, preferred_element_type=jnp.float32)
    pre_up = jnp.einsum("cnld,ldf->cnlf", token_rows, w_up, preferred_element_type=jnp.float32)
    grad_hidden = jnp.einsum(
        "cnld,lfd->cnlf", grad_rows, w_down, preferred_element_type=jnp.float32
    )
    own_terms = sum_at_owner(
        jnp.stack([pre_gate, pre_up, grad_hidden], 3).astype(jnp.bfloat16), "dp", 0
    )
    own_hidden, own_gate, own_up = swiglu_back(
        own_terms[:, :, :, 0], own_terms[:, :, :, 1], own_terms[:, :, :, 2]
    )
    hidden, gate_delta, up_delta = in_one_piece((own_hidden, own_gate, own_up), "dp", 0, 1)
    grad_down = jnp.einsum(
        "cnlf,cnld->lfd", hidden, grad_rows, preferred_element_type=jnp.float32
    ).astype(jnp.bfloat16)
    grad_gate = jnp.einsum(
        "cnld,cnlf->ldf", token_rows, gate_delta, preferred_element_type=jnp.float32
    ).astype(jnp.bfloat16)
    grad_up = jnp.einsum(
        "cnld,cnlf->ldf", token_rows, up_delta, preferred_element_type=jnp.float32
    ).astype(jnp.bfloat16)
    row_grad = jnp.einsum("cnlf,ldf->cnld", gate_delta, w_gate, preferred_element_type=jnp.float32)
    row_grad = row_grad + jnp.einsum(
        "cnlf,ldf->cnld", up_delta, w_up, preferred_element_type=jnp.float32
    )
    table_float = table_sum.astype(jnp.float32)
    column_part = sum_at_owner_2(row_grad, "tensor", 3)
    narrow = column_part.shape[3]
    back_cols = exchange_both(
        column_part.reshape(rows_all, EXPERTS, narrow),
        ("dp", "expert"),
        ("dp", "expert"),
        (0, 1),
        (2, 1),
    )
    token_part = jnp.dot(
        table_float.T,
        back_cols.reshape(capacity * EXPERTS, back_cols.shape[2]),
        precision=lax.Precision.HIGHEST,
        preferred_element_type=jnp.float32,
    )
    gathered_cols = lax.all_to_all(
        token_part.astype(jnp.bfloat16), "tensor", split_axis=0, concat_axis=1, tiled=True
    ).astype(token_part.dtype)
    replicas = back_cols.shape[2] // narrow
    tensor_count = gathered_cols.shape[1] // back_cols.shape[2]
    token_grad = gathered_cols.reshape(local_rows, tensor_count, replicas, narrow)
    token_grad = jnp.transpose(token_grad, (0, 2, 1, 3)).reshape(local_rows, model_width)
    return (token_grad.astype(jnp.bfloat16), grad_gate, grad_up, grad_down)


def solution(mesh):
    placed = (
        P(("dp", "expert", "tensor"), None),
        P(("dp", "expert", "tensor"), None),
        P(("dp", "expert"), None),
        P(("dp", "expert"), None),
        P(("dp", "expert"), None),
        P("expert", "dp", "tensor"),
        P("expert", "dp", "tensor"),
        P("expert", "tensor", "dp"),
    )
    return jax.shard_map(
        shards,
        mesh=mesh,
        in_specs=placed,
        out_specs=(
            P(("dp", "expert", "tensor"), None),
            P("expert", "dp", "tensor"),
            P("expert", "dp", "tensor"),
            P("expert", "tensor", "dp"),
        ),
        check_vma=False,
    )
```

profile of v0, /device:TPU:1, one launch (start us, length us, event | category | flops | bytes accessed | tf_op | source)
XLA Modules:
  0.0 383.0 jit_solution(18291135081032102056)
XLA Ops:
  7.2 1.7 pad_maximum_fusion.2
  10.4 30.1 %all-gather.3.cloned.1.call-done = bf16[64,8192]{1,0:T(8,128)(2,1)} async-done(((bf16[8,8192]{1,0:T(8,128)(2,1)}), bf16[64,8192]{1,0:T(8,128)(2,1)}) %all-gather.3.cloned.1.call-update) | async-done | bytes 1048592 | tf_op jit(solution)/shard_map/all_gather | solution.py:16
  40.5 1.7 fusion.30
  42.7 1.9 copy.56
  44.6 9.5 %all-to-all-start.1 = ((bf16[32,20,1,1024]{3,1,2,0:T(8,128)(2,1)}), bf16[32,20,1,1024]{3,1,2,0:T(8,128)(2,1)S(1)}, u32[]{:S(2)}, u32[]{:S(2)}) async-start(bf16[32,20,1,1024]{3,1,2,0:T(8,128)(2,1)} %bitcast.198), calls=%async_computation.1 | async-start | bytes 3145728 | tf_op jit(solution)/shard_map/all_to_all | solution.py:36
  55.7 1.9 copy.53
  57.6 34.3 %all-to-all-done.1 = bf16[32,20,1,1024]{3,1,2,0:T(8,128)(2,1)S(1)} async-done(((bf16[32,20,1,1024]{3,1,2,0:T(8,128)(2,1)}), bf16[32,20,1,1024]{3,1,2,0:T(8,128)(2,1)S(1)}, u32[]{:S(2)}, u32[]{:S(2)}) %all-to-all-start.1) | async-done | bytes 1310752 | tf_op jit(solution)/shard_map/all_to_all | solution.py:36
  91.9 6.5 %all-to-all-start = ((bf16[32,20,1,1024]{3,1,2,0:T(8,128)(2,1)}), bf16[32,20,1,1024]{3,1,2,0:T(8,128)(2,1)}, u32[]{:S(2)}, u32[]{:S(2)}) async-start(bf16[32,20,1,1024]{3,1,2,0:T(8,128)(2,1)} %bitcast.197), calls=%async_computation | async-start | bytes 3145728 | tf_op jit(solution)/shard_map/all_to_all | solution.py:36
  99.3 35.2 %all-to-all-done = bf16[32,20,1,1024]{3,1,2,0:T(8,128)(2,1)} async-done(((bf16[32,20,1,1024]{3,1,2,0:T(8,128)(2,1)}), bf16[32,20,1,1024]{3,1,2,0:T(8,128)(2,1)}, u32[]{:S(2)}, u32[]{:S(2)}) %all-to-all-start) | async-done | bytes 1310752 | tf_op jit(solution)/shard_map/all_to_all | solution.py:36
  134.5 2.1 copy.82
  142.4 81.7 %all_to_all.38 = bf16[4,20,8,1,3,896]{5,2,1,4,3,0:T(8,128)(2,1)S(1)} all-to-all(bf16[4,20,8,1,3,896]{5,2,1,4,3,0:T(8,128)(2,1)S(1)} %pad_maximum_fusion), channel_id=1, replica_groups=mesh['dp'=4,'expert'=8,'tensor'=8] {'dp'}, dimensions={0} | all-to-all | bytes 6881280 | tf_op jit(solution)/shard_map/all_to_all | solution.py:43
  225.9 65.6 %all-gather.5.cloned.1.call-done = bf16[80,24,1,896]{3,1,2,0:T(8,128)(2,1)} async-done(((bf16[20,24,1,896]{3,1,2,0:T(8,128)(2,1)}), bf16[80,24,1,896]{3,1,2,0:T(8,128)(2,1)}) %all-gather.5.cloned.1.call-update) | async-done | bytes 3440656 | tf_op jit(solution)/shard_map/all_gather | solution.py:16
  291.5 2.9 fusion.3
  294.4 2.8 add_bitcast_fusion
  297.3 1.7 copy.80
  299.0 10.9 %all-to-all-start.3 = ((f32[8,80,8,1,128]{4,2,1,3,0:T(8,128)}), f32[8,80,8,1,128]{4,2,1,3,0:T(8,128)}, u32[]{:S(2)}, u32[]{:S(2)}) async-start(f32[8,80,8,1,128]{4,2,1,3,0:T(8,128)} %bitcast.195), calls=%async_computation.3 | async-start | bytes 5242880 | tf_op jit(solution)/shard_map/all_to_all | solution.py:49
  309.9 4.7 %fusion.13 = bf16[1,1024,896]{2,1,0:T(8,128)(2,1)} fusion(bf16[80,8,1024]{2,1,0:T(8,128)(2,1)} %bitcast.208, bf16[80,24,1,896]{3,1,0,2:T(8,128)(2,1)} %bitcast.218), kind=kOutput, calls=%fused_computation.20 | convolution fusion | flops 1175322624 | bytes 4292608 | tf_op jit(solution)/shard_map/cnld,cnlf->ldf/dot_general | solution.py:122
  314.5 27.3 %all-to-all-done.3 = f32[8,80,8,1,128]{4,2,1,3,0:T(8,128)} async-done(((f32[8,80,8,1,128]{4,2,1,3,0:T(8,128)}), f32[8,80,8,1,128]{4,2,1,3,0:T(8,128)}, u32[]{:S(2)}, u32[]{:S(2)}) %all-to-all-start.3) | async-done | bytes 2621472 | tf_op jit(solution)/shard_map/all_to_all | solution.py:49
  341.8 1.9 reduce_sum.22
  344.8 6.8 %all-to-all-start.4 = ((f32[32,20,1,128]{3,2,1,0:T(1,128)}), f32[32,20,1,128]{3,2,1,0:T(1,128)S(1)}, u32[]{:S(2)}, u32[]{:S(2)}) async-start(f32[32,20,1,128]{3,2,1,0:T(1,128)} %copy.68), calls=%async_computation.4 | async-start | bytes 655360 | tf_op jit(solution)/shard_map/all_to_all | solution.py:36
  351.6 4.7 %fusion.14 = bf16[1,1024,896]{2,1,0:T(8,128)(2,1)} fusion(bf16[80,8,1024]{2,1,0:T(8,128)(2,1)} %bitcast.209, bf16[80,24,1,896]{3,1,0,2:T(8,128)(2,1)} %bitcast.219), kind=kOutput, calls=%fused_computation.21 | convolution fusion | flops 1175322624 | bytes 4292608 | tf_op jit(solution)/shard_map/cnld,cnlf->ldf/dot_general | solution.py:125
  356.3 7.8 %all-to-all-done.4 = f32[32,20,1,128]{3,2,1,0:T(1,128)S(1)} async-done(((f32[32,20,1,128]{3,2,1,0:T(1,128)}), f32[32,20,1,128]{3,2,1,0:T(1,128)S(1)}, u32[]{:S(2)}, u32[]{:S(2)}) %all-to-all-start.4) | async-done | bytes 327712 | tf_op jit(solution)/shard_map/all_to_all | solution.py:36
  365.1 5.6 %all-to-all-start.5 = ((bf16[8,8,512]{2,1,0:T(8,128)(2,1)}), bf16[8,8,512]{2,1,0:T(8,128)(2,1)S(1)}, u32[]{:S(2)}, u32[]{:S(2)}) async-start(bf16[8,8,512]{2,1,0:T(8,128)(2,1)} %fusion.25), calls=%async_computation.5 | async-start | bytes 131072 | tf_op jit(solution)/shard_map/all_to_all | solution.py:148
  370.6 4.1 %fusion.15 = bf16[1,896,1024]{2,1,0:T(8,128)(2,1)} fusion(bf16[80,8,1024]{2,1,0:T(8,128)(2,1)S(1)} %bitcast.205, bf16[80,24,1,896]{3,1,0,2:T(8,128)(2,1)} %bitcast.220), kind=kOutput, calls=%fused_computation.22 | convolution fusion | flops 1175322624 | bytes 4292608 | tf_op jit(solution)/shard_map/cnlf,cnld->lfd/dot_general | solution.py:119
  (36 shorter events, 15.3 us)
Async XLA Ops:
  7.2 129.6 %copy-start = (bf16[1,1024,896]{2,1,0:T(8,128)(2,1)S(1)}, bf16[1,1024,896]{2,1,0:T(8,128)(2,1)}, u32[]{:S(2)}) copy-start(bf16[1,1024,896]{2,1,0:T(8,128)(2,1)} %param.14) | copy-start | bytes 5505028
  7.2 33.3 %all-gather.3.cloned.1.call-start = ((), (), s32[]{:S(2)}) async-start(), calls=%async_computation.6 | async-start | bytes 1179648 | tf_op jit(solution)/shard_map/all_gather | solution.py:16
  40.5 1.7 copy-start.1
  44.6 47.3 %all-to-all-start.1 = ((bf16[32,20,1,1024]{3,1,2,0:T(8,128)(2,1)}), bf16[32,20,1,1024]{3,1,2,0:T(8,128)(2,1)S(1)}, u32[]{:S(2)}, u32[]{:S(2)}) async-start(bf16[32,20,1,1024]{3,1,2,0:T(8,128)(2,1)} %bitcast.198), calls=%async_computation.1 | async-start | bytes 3145728 | tf_op jit(solution)/shard_map/all_to_all | solution.py:36
  91.9 42.6 %all-to-all-start = ((bf16[32,20,1,1024]{3,1,2,0:T(8,128)(2,1)}), bf16[32,20,1,1024]{3,1,2,0:T(8,128)(2,1)}, u32[]{:S(2)}, u32[]{:S(2)}) async-start(bf16[32,20,1,1024]{3,1,2,0:T(8,128)(2,1)} %bitcast.197), calls=%async_computation | async-start | bytes 3145728 | tf_op jit(solution)/shard_map/all_to_all | solution.py:36
  98.4 193.0 %all-gather.5.cloned.1.call-start = ((), (), s32[]{:S(2)}) async-start(), calls=%async_computation.7 | async-start | bytes 4300800 | tf_op jit(solution)/shard_map/all_gather | solution.py:16
  136.8 1.6 copy-start.2
  136.8 2.0 copy-start.4
  138.8 1.5 copy-start.3
  291.5 3.0 copy-start.5
  299.0 42.8 %all-to-all-start.3 = ((f32[8,80,8,1,128]{4,2,1,3,0:T(8,128)}), f32[8,80,8,1,128]{4,2,1,3,0:T(8,128)}, u32[]{:S(2)}, u32[]{:S(2)}) async-start(f32[8,80,8,1,128]{4,2,1,3,0:T(8,128)} %bitcast.195), calls=%async_computation.3 | async-start | bytes 5242880 | tf_op jit(solution)/shard_map/all_to_all | solution.py:49
  344.8 19.3 %all-to-all-start.4 = ((f32[32,20,1,128]{3,2,1,0:T(1,128)}), f32[32,20,1,128]{3,2,1,0:T(1,128)S(1)}, u32[]{:S(2)}, u32[]{:S(2)}) async-start(f32[32,20,1,128]{3,2,1,0:T(1,128)} %copy.68), calls=%async_computation.4 | async-start | bytes 655360 | tf_op jit(solution)/shard_map/all_to_all | solution.py:36
  365.1 10.5 %all-to-all-start.5 = ((bf16[8,8,512]{2,1,0:T(8,128)(2,1)}), bf16[8,8,512]{2,1,0:T(8,128)(2,1)S(1)}, u32[]{:S(2)}, u32[]{:S(2)}) async-start(bf16[8,8,512]{2,1,0:T(8,128)(2,1)} %fusion.25), calls=%async_computation.5 | async-start | bytes 131072 | tf_op jit(solution)/shard_map/all_to_all | solution.py:148
Sparse Core Ops, SparseCore 0:
  10.4 29.9 all-gather.2
  226.0 65.3 all-gather.4
where the time goes:
time: 384 us; the launch traced here: 383 us
  waiting for transfers between devices  201 us (52%)
  blocking collectives  81.7 us (21%)
  starting transfers between devices  39.4 us (10%)
  matrix products  28.5 us (7%)
  between operations  14.3 us (4%)
  local copies, waits for them, and re-layouts  11.5 us (3%)
  other arithmetic  6.54 us (2%)
    all_gather x2, waiting for transfers between devices, in_one_piece(): lax.all_gather(both, axis, axis=dim, tiled=True)  95.6 us
    all_to_all x1, blocking collectives, sum_at_owner(): lax.all_to_all(pieces, axis, split_axis=0, concat_axis=0, tiled=True)  81.7 us
    all_to_all x3, waiting for transfers between devices, exchange_both(): lax.all_to_all(pieces, axis, split_axis=0, concat_axis=0, tiled=True)  77.4 us
    all_to_all x1, waiting for transfers between devices, sum_at_owner_2(): lax.all_to_all(pieces, axis, split_axis=0, concat_axis=0, tiled=True)  27.3 us
    all_to_all x3, starting transfers between devices, exchange_both(): lax.all_to_all(pieces, axis, split_axis=0, concat_axis=0, tiled=True)  22.8 us
    all_to_all x1, starting transfers between devices, sum_at_owner_2(): lax.all_to_all(pieces, axis, split_axis=0, concat_axis=0, tiled=True)  10.9 us
  transfers between devices with their start and end apart: 7, of which 7 were waited for; matrix products, arithmetic and copies ran while one was open for 5% of the time, Pallas kernels for 0%

commit v1 on v0

v1 whole, which is shorter than its diff:
```python
import functools

import jax
import jax.numpy as jnp
from jax import lax
from jax.experimental import pallas as pl
from jax.experimental.pallas import tpu as pltpu
from jax.sharding import PartitionSpec as P

BF, F32 = jnp.bfloat16, jnp.float32
MESH = pl.DeviceIdType.MESH
STAGES = 5
CAP, MAIN = 20, 16


def nt(a, b):
    return lax.dot_general(a, b, (((1,), (1,)), ((), ())), preferred_element_type=F32)


def nn(a, b):
    return jnp.dot(a, b, preferred_element_type=F32)


def remote(src, dst, send, recv, dev):
    return pltpu.make_async_remote_copy(
        src_ref=src, dst_ref=dst, send_sem=send, recv_sem=recv, device_id=dev, device_id_type=MESH
    )


def loop(n, f, start=0):
    def step(i, c):
        f(i)
        return c

    lax.fori_loop(start, n, step, 0)


def group_of(i):
    return lax.rem(2 * jnp.int32(i), jnp.int32(STAGES))


def kernel(
    sendA, tx, t0, t1, tt_ref, pp, wg_hbm, wu_hbm, wd_hbm,
    h_out, xg_out, y_out,
    wg, wu, wd, recvA, sendC, recvC, XG, part, rs1, raw, red, redS, H,
    rgp, recvP, qs, recvQ, zs, recvZ, sendY, recvY,
    wsem, sA, rA, sC, rC, sD, rD, sR, rR, sG, rG, sP, rP, sQ, rQ, sZ, rZ, sY, rY, osem,
):
    d, e, t = lax.axis_index("dp"), lax.axis_index("expert"), lax.axis_index("tensor")
    b = d * 8 + e
    core, y = lax.rem(t, 2), lax.div(t, 2)
    mate = t + 1 - 2 * core
    right, left, opp = lax.rem(d + 1, 4), lax.rem(d + 3, 4), lax.rem(d + 2, 4)

    def at_t(tt):
        return (d, e, tt)

    def at_p(p):
        return (lax.div(p, 8), lax.rem(p, 8), t)

    weights = [
        pltpu.make_async_copy(wg_hbm, wg, wsem.at[0]),
        pltpu.make_async_copy(wu_hbm, wu, wsem.at[1]),
        pltpu.make_async_copy(wd_hbm, wd, wsem.at[2]),
    ]
    for w in weights:
        w.start()

    bar = pltpu.get_barrier_semaphore()

    def greet_t(k):
        pl.semaphore_signal(bar, inc=1, device_id=at_t(lax.rem(t + k, 8)), device_id_type=MESH)

    def greet_p(k):
        pl.semaphore_signal(bar, inc=1, device_id=at_p(lax.rem(b + k, 32)), device_id_type=MESH)

    loop(32, greet_p, 1)
    loop(8, greet_t, 1)
    pl.semaphore_wait(bar, 38)

    def send_a(k):
        q = lax.rem(t + k, 8)
        return remote(sendA.at[q], recvA.at[t], sA.at[q], rA.at[t], at_t(q))

    loop(8, lambda k: send_a(k).start(), 1)
    recvA[t] = sendA[t]

    def wait_a(k):
        q = lax.rem(t + k, 8)
        remote(recvA.at[q], recvA.at[q], sA.at[q], rA.at[q], at_t(q)).wait_recv()

    loop(8, wait_a, 1)

    R = recvA[...].reshape(128, 512)
    xb = nn(tx[...], R).astype(BF)
    Rf = R.astype(F32)
    s0 = (pp[:, 0:1] * Rf).astype(BF)
    s1 = (pp[:, 1:2] * Rf).astype(BF)
    gb = (nn(t0[...], s0) + nn(t1[...], s1)).astype(BF)
    for dd in range(4):
        cols = slice(128 * dd, 128 * dd + 128)
        sendC[8 * dd : 8 * dd + 8, 0] = xb[:, cols].reshape(8, 32, 128)
        sendC[8 * dd : 8 * dd + 8, 1] = gb[:, cols].reshape(8, 32, 128)

    def send_c(k):
        p = lax.rem(b + k, 32)
        return remote(sendC.at[p], recvC.at[b], sC.at[p], rC.at[b], at_p(p))

    loop(32, lambda k: send_c(k).start(), 1)
    recvC[b] = sendC[b]

    def wait_c(p):
        @pl.when(p != b)
        def _():
            remote(recvC.at[p], recvC.at[p], sC.at[p], rC.at[p], at_p(p)).wait_recv()

    def piece(src, g):
        return XG.at[src, :, pl.ds(8 * g, 8)]

    def send_d(i, g, slot, src, dst):
        return remote(piece(src, g), piece(src, g), sD.at[i, slot], rD.at[i, src], at_t(dst))

    def wait_d(i, g, src):
        remote(piece(src, g), piece(src, g), sD.at[i, 0], rD.at[i, src], at_t(mate)).wait_recv()

    def prep_main(i):
        g = group_of(i)

        def one(j):
            p = 8 * g + j
            wait_c(p)
            XG[t, 0, p] = recvC[p, 0, 0:16]
            XG[t, 1, p] = recvC[p, 1, 0:16]

        loop(8, one)

    def start_d(i):
        g = group_of(i)
        send_d(i, g, 0, t, mate).start()
        for k in range(1, 4):
            send_d(i, g, k, t, lax.rem(t + 2 * k, 8)).start()

    def relay_d(i):
        g = group_of(i)
        for k in (1, 3, 2):
            q = lax.rem(t + 2 * k, 8)
            wait_d(i, g, q)
            send_d(i, g, 4 + k, q, mate).start()

    def arrive_d(i):
        g = group_of(i)
        for k in range(4):
            wait_d(i, g, lax.rem(mate + 2 * k, 8))

    for i in (0, 1, 3, 4):
        prep_main(i)
        start_d(i)

    def rest(j):
        for a in range(2):
            v = recvC[4 * j, a, 16:32].astype(F32)
            for q in range(1, 4):
                v = v + recvC[4 * j + q, a, 16:32].astype(F32)
            XG[t, a, 32 + j] = v.astype(BF)

    loop(8, rest)
    start_d(2)

    for w in weights:
        w.wait()

    def tile(g, owner, half):
        return 8 * g + 2 * owner + half

    def peer(dd):
        return (dd, e, t)

    def rs_send(i, m):
        g = group_of(i)
        src, dst, dev = {
            0: (part.at[:, tile(g, opp, 0)], rs1.at[0, i], right),
            1: (part.at[:, tile(g, right, 1)], raw.at[0, i], right),
            2: (redS.at[0, i], red.at[0, i], right),
            3: (part.at[:, tile(g, opp, 1)], rs1.at[1, i], left),
            4: (part.at[:, tile(g, left, 0)], raw.at[1, i], left),
            5: (redS.at[1, i], red.at[1, i], left),
        }[m]
        return remote(src, dst, sR.at[i, m], rR.at[i, m], peer(dev))

    def rs_wait(i, m):
        dst = (rs1, raw, red)[m % 3].at[m // 3, i]
        remote(dst, dst, sR.at[i, m], rR.at[i, m], peer(right)).wait_recv()

    def forward(i):
        @pl.when(i < STAGES - 1)
        def _():
            relay_d(i + 1)

        arrive_d(i)
        g = group_of(i)
        tiles = pl.ds(8 * g, 8)
        xs = jnp.concatenate([XG[q, 0, tiles].reshape(128, 128) for q in range(8)], axis=1)
        part[0, tiles] = nn(xs, wg[...]).astype(BF).reshape(8, 16, -1)
        part[1, tiles] = nn(xs, wu[...]).astype(BF).reshape(8, 16, -1)
        gs = jnp.concatenate([XG[q, 1, tiles].reshape(128, 128) for q in range(8)], axis=1)
        part[2, tiles] = nt(gs, wd[...]).astype(BF).reshape(8, 16, -1)
        for m in (0, 3, 1, 4):
            rs_send(i, m).start()

    relay_d(0)
    loop(STAGES, forward)

    outs = [
        pltpu.make_async_copy(XG.at[q], xg_out.at[:, :, :, pl.ds(128 * q, 128)], osem.at[q])
        for q in range(8)
    ]
    for o in outs:
        o.start()

    def middle(i):
        g = group_of(i)
        rs_wait(i, 0)
        redS[0, i] = (part[:, tile(g, right, 0)].astype(F32) + rs1[0, i].astype(F32)).astype(BF)
        rs_send(i, 2).start()
        rs_wait(i, 3)
        redS[1, i] = (part[:, tile(g, left, 1)].astype(F32) + rs1[1, i].astype(F32)).astype(BF)
        rs_send(i, 5).start()

    loop(STAGES, middle)

    def ag_send(i, m):
        g = group_of(i)
        src, dev = {
            0: (H.at[:, pl.ds(tile(g, d, 0), 2)], right),
            1: (H.at[:, pl.ds(tile(g, d, 0), 2)], left),
            2: (H.at[:, tile(g, left, 0)], right),
            3: (H.at[:, tile(g, right, 1)], left),
        }[m]
        return remote(src, src, sG.at[i, m], rG.at[i, m], peer(dev))

    def ag_wait(i, m):
        g = group_of(i)
        dst = (
            H.at[:, pl.ds(tile(g, left, 0), 2)],
            H.at[:, pl.ds(tile(g, right, 0), 2)],
            H.at[:, tile(g, opp, 0)],
            H.at[:, tile(g, opp, 1)],
        )[m]
        remote(dst, dst, sG.at[i, m], rG.at[i, m], peer(right)).wait_recv()

    def own(i):
        g = group_of(i)
        rs_wait(i, 1)
        rs_wait(i, 4)
        for half, (ra, rb, m) in enumerate(((red, raw, 2), (raw, red, 5))):
            rs_wait(i, m)
            at = tile(g, d, half)
            pre = [
                part[u, at].astype(F32) + ra[0, i, u].astype(F32) + rb[1, i, u].astype(F32)
                for u in range(3)
            ]
            gate, up, grad = pre
            s = jax.nn.sigmoid(gate)
            silu = gate * s
            H[0, at] = (silu * up).astype(BF)
            H[1, at] = (grad * up * s * (1.0 + gate * (1.0 - s))).astype(BF)
            H[2, at] = (grad * silu).astype(BF)
        ag_send(i, 0).start()
        ag_send(i, 1).start()

    loop(STAGES, own)

    def relay(i):
        ag_wait(i, 0)
        ag_send(i, 2).start()
        ag_wait(i, 1)
        ag_send(i, 3).start()

    loop(STAGES, relay)

    def p_copy(i):
        return remote(rgp.at[i, 1 - core], recvP.at[i], sP.at[i], rP.at[i], at_t(mate))

    def q_send(i, k):
        yy = lax.rem(y + k, 4)
        return remote(qs.at[i, yy], recvQ.at[i, y], sQ.at[i, yy], rQ.at[i, y], at_t(2 * yy + core))

    def rows(i):
        ag_wait(i, 2)
        ag_wait(i, 3)
        g = group_of(i)
        tiles = pl.ds(8 * g, 8)
        rg = nt(H[1, tiles].reshape(128, -1), wg[...]) + nt(H[2, tiles].reshape(128, -1), wu[...])
        for q in range(8):
            rgp[i, q % 2, q // 2] = rg[:, 128 * q : 128 * q + 128].astype(BF)
        p_copy(i).start()

    def pair(i):
        remote(recvP.at[i], recvP.at[i], sP.at[i], rP.at[i], at_t(mate)).wait_recv()
        qs[i] = (rgp[i, core].astype(F32) + recvP[i].astype(F32)).astype(BF)
        for k in (2, 1, 3):
            q_send(i, k).start()

    def z_main(i, j):
        p = 8 * group_of(i) + j
        return p, remote(zs.at[i, j], recvZ.at[b, 0], sZ.at[0, p], rZ.at[0, b], at_p(p))

    def z_rest(p):
        return remote(zs.at[2, lax.div(p, 4)], recvZ.at[b, 1], sZ.at[1, p], rZ.at[1, b], at_p(p))

    def back(i):
        tot = qs[i, y].astype(F32)
        for k in range(1, 4):
            yy = lax.rem(y + k, 4)
            remote(recvQ.at[i, yy], recvQ.at[i, yy], sQ.at[i, yy], rQ.at[i, yy], at_t(mate)).wait_recv()
            tot = tot + recvQ[i, yy].astype(F32)
        zs[i] = tot.astype(BF).reshape(8, 16, 128)

        @pl.when(group_of(i) < 4)
        def _():
            def one(j):
                p, copy = z_main(i, j)

                @pl.when(p != b)
                def _():
                    copy.start()

                @pl.when(p == b)
                def _():
                    recvZ[b, 0] = zs[i, j]

            loop(8, one)

        @pl.when(group_of(i) == 4)
        def _():
            loop(32, lambda k: z_rest(lax.rem(b + k, 32)).start(), 1)
            recvZ[b, 1] = zs[2, lax.div(b, 4)]

    def finish(i):
        rows(i)

        @pl.when(i >= 1)
        def _():
            pair(i - 1)

        @pl.when(i >= 2)
        def _():
            back(i - 2)

    loop(STAGES, finish)
    houts = [pltpu.make_async_copy(H, h_out, osem.at[8])]
    for o in houts:
        o.start()
    pair(STAGES - 1)
    back(STAGES - 2)
    back(STAGES - 1)

    def wait_z(k):
        p = lax.rem(b + k, 32)
        for w in range(2):
            remote(recvZ.at[p, w], recvZ.at[p, w], sZ.at[w, p], rZ.at[w, p], at_p(p)).wait_recv()

    loop(32, wait_z, 1)
    for dd in range(4):
        z = recvZ[8 * dd : 8 * dd + 8].reshape(256, 128)
        sendY[:, :, 128 * dd : 128 * dd + 128] = nn(tt_ref[...], z).astype(BF).reshape(8, 16, 128)

    def y_copy(k):
        q = lax.rem(t + k, 8)
        return remote(sendY.at[q], recvY.at[t], sY.at[q], rY.at[t], at_t(q))

    loop(8, lambda k: y_copy(k).start(), 1)
    recvY[t] = sendY[t]

    def wait_y(k):
        q = lax.rem(t + k, 8)
        remote(recvY.at[q], recvY.at[q], sY.at[q], rY.at[q], at_t(q)).wait_recv()

    loop(8, wait_y, 1)
    y_out[...] = recvY[...]

    loop(8, lambda k: send_a(k).wait_send(), 1)
    loop(32, lambda k: send_c(k).wait_send(), 1)

    def drain(i):
        g = group_of(i)
        send_d(i, g, 0, t, mate).wait_send()
        for k in range(1, 4):
            send_d(i, g, k, t, mate).wait_send()
            send_d(i, g, 4 + k, t, mate).wait_send()
        for m in range(6):
            rs_send(i, m).wait_send()
        for m in range(4):
            ag_send(i, m).wait_send()
        p_copy(i).wait_send()
        for k in range(1, 4):
            q_send(i, k).wait_send()

        @pl.when(g < 4)
        def _():
            def one(j):
                p, copy = z_main(i, j)

                @pl.when(p != b)
                def _():
                    copy.wait_send()

            loop(8, one)

    loop(STAGES, drain)
    loop(32, lambda k: z_rest(lax.rem(b + k, 32)).wait_send(), 1)
    loop(8, lambda k: y_copy(k).wait_send(), 1)
    for o in outs + houts:
        o.wait()


def tables(route_probs, expert_ids, slot_index):
    e = lax.axis_index("expert")
    row = jnp.where(slot_index < MAIN, slot_index, slot_index + 4 * lax.rem(e, 4))
    place = jnp.where(slot_index < CAP, expert_ids * 32 + row, -1)
    place = place.T.reshape(2, 8, 8)
    none = jnp.full_like(place, -1)
    at_x = jnp.concatenate([place, none], axis=2).reshape(2, 128)
    at_g = jnp.concatenate([none, place], axis=2).reshape(2, 128)
    places = jnp.arange(256, dtype=jnp.int32)
    tx = ((places[:, None] == at_x[0]) | (places[:, None] == at_x[1])).astype(BF)
    tt = ((places == at_x[0][:, None]) | (places == at_x[1][:, None])).astype(BF)
    t0 = (places[:, None] == at_g[0]).astype(BF)
    t1 = (places[:, None] == at_g[1]).astype(BF)
    probs = route_probs.reshape(8, 8, 2)
    probs = jnp.concatenate([jnp.zeros_like(probs), probs], axis=1).reshape(128, 2)
    return tx, t0, t1, tt, probs


def shards(tokens, out_grad, route_probs, expert_ids, slot_index, w_gate, w_up, w_down):
    tx, t0, t1, tt, probs = tables(route_probs, expert_ids, slot_index)
    both = jnp.stack([tokens, out_grad], 0).reshape(2, 8, 4, 8, 128)
    both = jnp.transpose(both, (3, 0, 1, 2, 4)).reshape(8, 16, 512)
    wg, wu, wd = w_gate[0], w_up[0], w_down[0]
    dl, fl = wg.shape
    vm = pl.BlockSpec(memory_space=pltpu.VMEM)
    hbm = pl.BlockSpec(memory_space=pl.ANY)
    S = STAGES
    dma = pltpu.SemaphoreType.DMA
    h, xg, yv = pl.pallas_call(
        kernel,
        name="expert_back",
        out_shape=(
            jax.ShapeDtypeStruct((3, 40, 16, fl), BF),
            jax.ShapeDtypeStruct((2, 40, 16, dl), BF),
            jax.ShapeDtypeStruct((8, 16, 512), BF),
        ),
        in_specs=[vm] * 6 + [hbm] * 3,
        out_specs=(hbm, hbm, vm),
        scratch_shapes=[
            pltpu.VMEM((dl, fl), BF),
            pltpu.VMEM((dl, fl), BF),
            pltpu.VMEM((fl, dl), BF),
            pltpu.VMEM((8, 16, 512), BF),
            pltpu.VMEM((32, 2, 32, 128), BF),
            pltpu.VMEM((32, 2, 32, 128), BF),
            pltpu.VMEM((8, 2, 40, 16, 128), BF),
            pltpu.VMEM((3, 40, 16, fl), BF),
            pltpu.VMEM((2, S, 3, 16, fl), BF),
            pltpu.VMEM((2, S, 3, 16, fl), BF),
            pltpu.VMEM((2, S, 3, 16, fl), BF),
            pltpu.VMEM((2, S, 3, 16, fl), BF),
            pltpu.VMEM((3, 40, 16, fl), BF),
            pltpu.VMEM((S, 2, 4, 128, 128), BF),
            pltpu.VMEM((S, 4, 128, 128), BF),
            pltpu.VMEM((S, 4, 128, 128), BF),
            pltpu.VMEM((S, 4, 128, 128), BF),
            pltpu.VMEM((S, 8, 16, 128), BF),
            pltpu.VMEM((32, 2, 16, 128), BF),
            pltpu.VMEM((8, 16, 512), BF),
            pltpu.VMEM((8, 16, 512), BF),
            dma((3,)), dma((8,)), dma((8,)), dma((32,)), dma((32,)),
            dma((S, 8)), dma((S, 8)), dma((S, 6)), dma((S, 6)), dma((S, 4)), dma((S, 4)),
            dma((S,)), dma((S,)), dma((S, 4)), dma((S, 4)), dma((2, 32)), dma((2, 32)),
            dma((8,)), dma((8,)), dma((9,)),
        ],
        compiler_params=pltpu.CompilerParams(
            collective_id=0, has_side_effects=True, vmem_limit_bytes=60 * 1024 * 1024
        ),
    )(both, tx, t0, t1, tt, probs, wg, wu, wd)
    h = h.reshape(3, 640, fl)
    xg = xg.reshape(2, 640, dl)

    def tn(a, c):
        return lax.dot_general(a, c, (((0,), (0,)), ((), ())), preferred_element_type=F32).astype(BF)[None]

    grad_down = tn(h[0], xg[1])
    grad_gate = tn(xg[0], h[1])
    grad_up = tn(xg[0], h[2])
    token_grad = yv[:, :8].reshape(8, 8, 4, 128)
    token_grad = jnp.transpose(token_grad, (1, 2, 0, 3)).reshape(8, 4096)
    return token_grad, grad_gate, grad_up, grad_down


def solution(mesh):
    placed = (
        P(("dp", "expert", "tensor"), None),
        P(("dp", "expert", "tensor"), None),
        P(("dp", "expert"), None),
        P(("dp", "expert"), None),
        P(("dp", "expert"), None),
        P("expert", "dp", "tensor"),
        P("expert", "dp", "tensor"),
        P("expert", "tensor", "dp"),
    )
    return jax.shard_map(
        shards,
        mesh=mesh,
        in_specs=placed,
        out_specs=(
            P(("dp", "expert", "tensor"), None),
            P("expert", "dp", "tensor"),
            P("expert", "dp", "tensor"),
            P("expert", "tensor", "dp"),
        ),
        check_vma=False,
    )
```

time: 384 us -> 199 us (0.52)
  waiting for transfers between devices: 201 us -> 0 us
  Pallas kernels: 0 us -> 180 us
  blocking collectives: 81.7 us -> 0 us
  starting transfers between devices: 39.4 us -> 0 us
  matrix products: 28.5 us -> 10.7 us
  between operations: 14.3 us -> 0.66 us
  local copies, waits for them, and re-layouts: 11.5 us -> 3.38 us
    pallas_call x0 -> x1, Pallas kernels: none -> 180 us  [shards(): pl.pallas_call(kernel, name='expert_back', out_shape=(jax.ShapeDtypeStruc...]
    all_to_all x5 -> x0, waiting for transfers between devices: 105 us -> none  [the longest x3 77.4 us: exchange_both(): lax.all_to_all(pieces, axis, split_axis=0, concat_axis=0, tiled=True)]
    all_gather x2 -> x0, waiting for transfers between devices: 95.6 us -> none  [in_one_piece(): lax.all_gather(both, axis, axis=dim, tiled=True)]
    all_to_all x1 -> x0, blocking collectives: 81.7 us -> none  [sum_at_owner(): lax.all_to_all(pieces, axis, split_axis=0, concat_axis=0, tiled=True)]
    all_to_all x5 -> x0, starting transfers between devices: 39.3 us -> none  [the longest x3 22.8 us: exchange_both(): lax.all_to_all(pieces, axis, split_axis=0, concat_axis=0, tiled=True)]
    dot_general x12 -> x3, matrix products: 28.5 us -> 10.7 us  [tn(): lax.dot_general(a, c, (((0,), (0,)), ((), ())), preferred_element_type=F32)]
  transfers between devices with their start and end apart: 7 -> 0, of which waited for: 7 -> 0; matrix products, arithmetic and copies ran while one was open for 5% -> 0% of each run, Pallas kernels for 0% -> 0%
where the time goes in v1:
time: 199 us
  Pallas kernels  180 us (90%)
  matrix products  10.7 us (5%)
  other arithmetic  4.3 us (2%)
  local copies, waits for them, and re-layouts  3.38 us (2%)
    pallas_call x1, Pallas kernels, shards(): pl.pallas_call(kernel, name='expert_back', out_shape=(jax.ShapeDtypeStruc...  180 us
    dot_general x3, matrix products, tn(): lax.dot_general(a, c, (((0,), (0,)), ((), ())), preferred_element_type=F32)  10.7 us

profile of v1, /device:TPU:1, one launch (start us, length us, event | category | flops | bytes accessed | tf_op | source)
XLA Modules:
  0.0 199.0 jit_solution(18190528204037067077)
XLA Ops:
  0.6 0.7 fusion.21
  1.3 0.1 reshape.74
  1.4 0.1 pad_slice_fusion
  1.5 0.1 eq.99
  1.6 0.1 eq.91
  1.7 0.1 eq.87
  1.7 0.1 eq.95
  1.8 0.8 copy.30
  2.6 0.6 concatenate.12.clone
  3.2 0.6 fusion.18.t1
  3.9 0.7 fusion.20.tt_ref
  4.6 0.7 fusion.16
  5.3 1.5 copy_bitcast_fusion.sendA
  6.8 179.9 %expert_back.1 = (bf16[3,40,16,896]{3,2,1,0:T(8,128)(2,1)}, bf16[2,40,16,1024]{3,2,1,0:T(8,128)(2,1)}, bf16[8,16,512]{2,1,0:T(8,128)(2,1)}) custom-call(bf16[8,16,512]{2,1,0:T(8,128)(2,1)} %copy_bitcast_fusion.sendA, bf16[256,128]{1,0:T(8,128)(2,1)} %get-tuple-element.14.tx, bf16[256,128]{1,0:T(8,128)(2,1)} %get-tuple-element.15.t0, ...), custom_call_target="tpu_custom_call" | custom-call | tf_op jit(solution)/shard_map/expert_back/pallas_call | solution.py:445
  186.8 0.8 slice_bitcast_fusion
  187.6 0.6 copy.15
  188.3 0.0 copy-start
  188.3 0.0 copy-start.1
  188.3 4.8 %fusion.1 = bf16[1,1024,896]{2,1,0:T(8,128)(2,1)} fusion(bf16[2,40,16,1024]{3,2,1,0:T(8,128)(2,1)} %get-tuple-element.8, bf16[3,40,16,896]{3,2,1,0:T(8,128)(2,1)} %get-tuple-element.9), kind=kOutput, calls=%fused_computation.4 | convolution fusion | flops 1175322624 | bytes 4292608 | tf_op jit(solution)/shard_map/dot_general | solution.py:490
  193.1 0.0 copy-done
  193.1 0.0 copy-done.1
  193.1 2.9 %fusion.2 = bf16[1,896,1024]{2,1,0:T(8,128)(2,1)} fusion(bf16[2,40,16,1024]{3,2,1,0:T(8,128)(2,1)S(1)} %copy-done.1, bf16[3,40,16,896]{3,2,1,0:T(8,128)(2,1)S(1)} %copy-done), kind=kOutput, calls=%fused_computation.5 | convolution fusion | flops 1175322624 | bytes 4292608 | tf_op jit(solution)/shard_map/dot_general | solution.py:490
  196.0 3.0 %fusion = bf16[1,1024,896]{2,1,0:T(8,128)(2,1)} fusion(bf16[2,40,16,1024]{3,2,1,0:T(8,128)(2,1)S(1)} %copy-done.1, bf16[3,40,16,896]{3,2,1,0:T(8,128)(2,1)S(1)} %copy-done), kind=kOutput, calls=%fused_computation.3 | convolution fusion | flops 1175322624 | bytes 4292608 | tf_op jit(solution)/shard_map/dot_general | solution.py:490
Async XLA Ops:
  188.3 4.8 %copy-start = (bf16[3,40,16,896]{3,2,1,0:T(8,128)(2,1)S(1)}, bf16[3,40,16,896]{3,2,1,0:T(8,128)(2,1)}, u32[]{:S(2)}) copy-start(bf16[3,40,16,896]{3,2,1,0:T(8,128)(2,1)} %get-tuple-element.9) | copy-start | bytes 10321924
  188.3 4.8 %copy-start.1 = (bf16[2,40,16,1024]{3,2,1,0:T(8,128)(2,1)S(1)}, bf16[2,40,16,1024]{3,2,1,0:T(8,128)(2,1)}, u32[]{:S(2)}) copy-start(bf16[2,40,16,1024]{3,2,1,0:T(8,128)(2,1)} %get-tuple-element.8) | copy-start | bytes 7864324

commit v2 on v1

v2 whole, which is shorter than its diff:
```python
import jax
import jax.numpy as jnp
from jax import lax
from jax.experimental import pallas as pl
from jax.experimental.pallas import tpu as pltpu
from jax.sharding import PartitionSpec as P

BF, F32 = jnp.bfloat16, jnp.float32
MESH = pl.DeviceIdType.MESH
S = 5
CAP = 20
PLACES = 192


def nt(a, b):
    return lax.dot_general(a, b, (((1,), (1,)), ((), ())), preferred_element_type=F32)


def tn(a, b):
    return lax.dot_general(a, b, (((0,), (0,)), ((), ())), preferred_element_type=F32)


def nn(a, b):
    return jnp.dot(a, b, preferred_element_type=F32)


def remote(src, dst, send, recv, dev):
    return pltpu.make_async_remote_copy(
        src_ref=src, dst_ref=dst, send_sem=send, recv_sem=recv, device_id=dev, device_id_type=MESH
    )


def loop(n, f, start=0):
    def step(i, c):
        f(i)
        return c

    lax.fori_loop(start, n, step, 0)


def column(row):
    n = row.shape[1]
    eye = lax.broadcasted_iota(jnp.int32, (n, n), 0) == lax.broadcasted_iota(jnp.int32, (n, n), 1)
    spread = jnp.where(eye, jnp.broadcast_to(row, (n, n)), jnp.zeros((n, n), row.dtype))
    return jnp.sum(spread, axis=1, keepdims=True)


def kernel(
    tok_hbm, og_hbm, prob_hbm, id_hbm, slot_hbm, wg_hbm, wu_hbm, wd_hbm,
    y_out, gg_out, gu_out, gd_out,
    tok, og, prob, ids, slots, wg, wu, wd, tab,
    sendA, recvA, sendC, recvC, XG, XT, part, rs1, raw, red, redS, H,
    rgp, recvP, qs, recvQ, zs, recvZ, sendY, recvY, accg, accd, outg, outd,
    isem, wsem, sA, rA, sC, rC, sD, rD, sR, rR, sG, rG, sP, rP, sQ, rQ, sZ, rZ, sY, rY, osem,
):
    d, e, t = lax.axis_index("dp"), lax.axis_index("expert"), lax.axis_index("tensor")
    b = d * 8 + e
    core, y = lax.rem(t, 2), lax.div(t, 2)
    mate = t + 1 - 2 * core
    right, left, opp = lax.rem(d + 1, 4), lax.rem(d + 3, 4), lax.rem(d + 2, 4)

    def at_t(tt):
        return (d, e, tt)

    def at_p(p):
        return (lax.div(p, 8), lax.rem(p, 8), t)

    bar = pltpu.get_barrier_semaphore()

    def greet_t(k):
        pl.semaphore_signal(bar, inc=1, device_id=at_t(lax.rem(t + k, 8)), device_id_type=MESH)

    def greet_p(k):
        pl.semaphore_signal(bar, inc=1, device_id=at_p(lax.rem(b + k, 32)), device_id_type=MESH)

    loop(32, greet_p, 1)
    loop(8, greet_t, 1)

    inputs = [
        pltpu.make_async_copy(src, dst, isem.at[n])
        for n, (src, dst) in enumerate(
            ((tok_hbm, tok), (og_hbm, og), (prob_hbm, prob), (id_hbm, ids), (slot_hbm, slots))
        )
    ]
    weights = [
        pltpu.make_async_copy(src, dst, wsem.at[n])
        for n, (src, dst) in enumerate(((wg_hbm, wg), (wu_hbm, wu), (wd_hbm, wd)))
    ]
    for c in inputs + weights:
        c.start()
    for c in inputs:
        c.wait()
    for dd in range(4):
        for q in range(8):
            at = slice(1024 * dd + 128 * q, 1024 * dd + 128 * q + 128)
            sendA[q, 0, :, 128 * dd : 128 * dd + 128] = tok[:, at]
            sendA[q, 1, :, 128 * dd : 128 * dd + 128] = og[:, at]
    slot, owner = slots[...], ids[...] * 8
    place = jnp.where(
        slot >= 16,
        owner + 4 * lax.rem(e, 2) + slot - 16,
        jnp.where(slot < 8, 64 + owner + slot, 120 + owner + slot),
    )
    place = jnp.where(slot < CAP, place, -1)
    by_place = lax.broadcasted_iota(jnp.int32, (PLACES, 64), 0)
    t0, t1 = ((by_place == place[k : k + 1]).astype(F32) for k in range(2))
    tx, t0, t1 = (t0 + t1).astype(BF), t0.astype(BF), t1.astype(BF)
    by_token = lax.broadcasted_iota(jnp.int32, (64, PLACES), 1)
    tab[...] = sum((by_token == column(place[k : k + 1])).astype(F32) for k in range(2)).astype(BF)
    p0, p1 = (column(prob[k : k + 1]) for k in range(2))
    pl.semaphore_wait(bar, 38)

    def send_a(k):
        q = lax.rem(t + k, 8)
        return remote(sendA.at[q], recvA.at[t], sA.at[q], rA.at[t], at_t(q))

    loop(8, lambda k: send_a(k).start(), 1)
    recvA[t] = sendA[t]

    def wait_a(k):
        q = lax.rem(t + k, 8)
        remote(recvA.at[q], recvA.at[q], sA.at[q], rA.at[q], at_t(q)).wait_recv()

    loop(8, wait_a, 1)

    rx = recvA[:, 0].astype(F32).reshape(64, 512).astype(BF)
    ry = recvA[:, 1].astype(F32).reshape(64, 512)
    xb = nn(tx, rx)
    gb = nn(t0, (p0 * ry).astype(BF)) + nn(t1, (p1 * ry).astype(BF))
    for c in range(3):
        for dd in range(4):
            cut = slice(64 * c, 64 * c + 64), slice(128 * dd, 128 * dd + 128)
            for a, v in enumerate((xb, gb)):
                sendC[c, 8 * dd : 8 * dd + 8, a] = v[cut].reshape(8, 8, 128).astype(BF)

    def send_c(c, k):
        p = lax.rem(b + k, 32)
        return remote(sendC.at[c, p], recvC.at[c, b], sC.at[c, p], rC.at[c, b], at_p(p))

    for c in range(3):
        loop(32, lambda k, c=c: send_c(c, k).start(), 1)
        recvC[c, b] = sendC[c, b]

    def wait_c(c, p):
        @pl.when(p != b)
        def _():
            ref = recvC.at[c, p]
            remote(ref, ref, sC.at[c, p], rC.at[c, p], at_p(p)).wait_recv()

    def piece(src, i):
        return XG.at[src, :, pl.ds(8 * i, 8)]

    def send_d(i, slot, src, dst):
        return remote(piece(src, i), piece(src, i), sD.at[i, slot], rD.at[i, src], at_t(dst))

    def wait_d(i, src):
        remote(piece(src, i), piece(src, i), sD.at[i, 0], rD.at[i, src], at_t(mate)).wait_recv()

    def octet(c, p, a):
        return recvC[c, p, a].astype(F32)

    def start_d(i):
        send_d(i, 0, t, mate).start()
        for k in range(1, 4):
            send_d(i, k, t, lax.rem(t + 2 * k, 8)).start()

    def relay_d(i):
        for k in (1, 3, 2):
            q = lax.rem(t + 2 * k, 8)
            wait_d(i, q)
            send_d(i, 4 + k, q, mate).start()

    def arrive_d(i):
        for k in range(4):
            wait_d(i, lax.rem(mate + 2 * k, 8))

    loop(32, lambda p: wait_c(0, p))

    def rest(j):
        for a in range(2):
            lo = octet(0, 4 * j, a) + octet(0, 4 * j + 1, a)
            hi = octet(0, 4 * j + 2, a) + octet(0, 4 * j + 3, a)
            XG[t, a, j] = jnp.concatenate([lo, hi], axis=0).astype(BF)

    loop(8, rest)
    start_d(0)

    def prep(i):
        c, first = lax.div(i + 1, 2), 16 * lax.rem(i + 1, 2)

        def one(j):
            p = first + 2 * j
            wait_c(c, p)
            wait_c(c, p + 1)
            for a in range(2):
                both = jnp.concatenate([octet(c, p, a), octet(c, p + 1, a)], axis=0)
                XG[t, a, 8 * i + j] = both.astype(BF)

        loop(8, one)
        start_d(i)

    def tile(i, owner, half):
        return 8 * i + 2 * owner + half

    def peer(dd):
        return (dd, e, t)

    def rs_send(i, m):
        src, dst, dev = {
            0: (part.at[:, tile(i, opp, 0)], rs1.at[0, i], right),
            1: (part.at[:, tile(i, right, 1)], raw.at[0, i], right),
            2: (redS.at[0, i], red.at[0, i], right),
            3: (part.at[:, tile(i, opp, 1)], rs1.at[1, i], left),
            4: (part.at[:, tile(i, left, 0)], raw.at[1, i], left),
            5: (redS.at[1, i], red.at[1, i], left),
        }[m]
        return remote(src, dst, sR.at[i, m], rR.at[i, m], peer(dev))

    def rs_wait(i, m):
        dst = (rs1, raw, red)[m % 3].at[m // 3, i]
        remote(dst, dst, sR.at[i, m], rR.at[i, m], peer(right)).wait_recv()

    def rows_of(a, i):
        tiles = pl.ds(8 * i, 8)
        return jnp.concatenate([XG[q, a, tiles].reshape(128, 128) for q in range(8)], axis=1)

    def forward(i):
        tiles = pl.ds(8 * i, 8)
        xs = rows_of(0, i)
        part[0, tiles] = nn(xs, wg[...]).astype(BF).reshape(8, 16, -1)
        part[1, tiles] = nn(xs, wu[...]).astype(BF).reshape(8, 16, -1)
        part[2, tiles] = nt(rows_of(1, i), wd[...]).astype(BF).reshape(8, 16, -1)
        for m in (0, 3, 1, 4):
            rs_send(i, m).start()

    for c in weights:
        c.wait()

    def open_stage(i):
        @pl.when(i < S - 1)
        def _():
            prep(i + 1)

        relay_d(i)
        arrive_d(i)
        forward(i)

    loop(S, open_stage)

    def middle(i):
        rs_wait(i, 0)
        redS[0, i] = (part[:, tile(i, right, 0)].astype(F32) + rs1[0, i].astype(F32)).astype(BF)
        rs_send(i, 2).start()
        rs_wait(i, 3)
        redS[1, i] = (part[:, tile(i, left, 1)].astype(F32) + rs1[1, i].astype(F32)).astype(BF)
        rs_send(i, 5).start()

    loop(S, middle)

    def ag_send(i, m):
        src, dev = {
            0: (H.at[:, pl.ds(tile(i, d, 0), 2)], right),
            1: (H.at[:, pl.ds(tile(i, d, 0), 2)], left),
            2: (H.at[:, tile(i, left, 0)], right),
            3: (H.at[:, tile(i, right, 1)], left),
        }[m]
        return remote(src, src, sG.at[i, m], rG.at[i, m], peer(dev))

    def ag_wait(i, m):
        dst = (
            H.at[:, pl.ds(tile(i, left, 0), 2)],
            H.at[:, pl.ds(tile(i, right, 0), 2)],
            H.at[:, tile(i, opp, 0)],
            H.at[:, tile(i, opp, 1)],
        )[m]
        remote(dst, dst, sG.at[i, m], rG.at[i, m], peer(right)).wait_recv()

    def own(i):
        rs_wait(i, 1)
        rs_wait(i, 4)
        for half, (ra, rb, m) in enumerate(((red, raw, 2), (raw, red, 5))):
            rs_wait(i, m)
            at = tile(i, d, half)
            gate, up, grad = (
                part[u, at].astype(F32) + ra[0, i, u].astype(F32) + rb[1, i, u].astype(F32)
                for u in range(3)
            )
            s = jax.nn.sigmoid(gate)
            silu = gate * s
            H[0, at] = (silu * up).astype(BF)
            H[1, at] = (grad * up * s * (1.0 + gate * (1.0 - s))).astype(BF)
            H[2, at] = (grad * silu).astype(BF)
        ag_send(i, 0).start()
        ag_send(i, 1).start()

    def relay(i):
        ag_wait(i, 0)
        ag_send(i, 2).start()
        ag_wait(i, 1)
        ag_send(i, 3).start()

    def p_copy(i):
        return remote(rgp.at[i, 1 - core], recvP.at[i], sP.at[i], rP.at[i], at_t(mate))

    def q_send(i, k):
        yy = lax.rem(y + k, 4)
        return remote(qs.at[i, yy], recvQ.at[i, y], sQ.at[i, yy], rQ.at[i, y], at_t(2 * yy + core))

    def hid(u, i):
        return H[u, pl.ds(8 * i, 8)].reshape(128, -1)

    def rows(i):
        ag_wait(i, 2)
        ag_wait(i, 3)
        rg = nt(hid(1, i), wg[...]) + nt(hid(2, i), wu[...])
        for q in range(8):
            rgp[i, q % 2, q // 2] = rg[:, 128 * q : 128 * q + 128].astype(BF)
        p_copy(i).start()

    def pair(i):
        remote(recvP.at[i], recvP.at[i], sP.at[i], rP.at[i], at_t(mate)).wait_recv()
        qs[i] = (rgp[i, core].astype(F32) + recvP[i].astype(F32)).astype(BF)
        for k in (2, 1, 3):
            q_send(i, k).start()

    def z_main(i, o):
        c, p = lax.div(i + 1, 2), 16 * lax.rem(i + 1, 2) + o
        return c, p, remote(zs.at[i, o], recvZ.at[c, b], sZ.at[c, p], rZ.at[c, b], at_p(p))

    def z_rest(p):
        return remote(zs.at[0, lax.div(p, 2)], recvZ.at[0, b], sZ.at[0, p], rZ.at[0, b], at_p(p))

    def back(i):
        tot = qs[i, y].astype(F32)
        for k in (1, 3, 2):
            yy = lax.rem(y + k, 4)
            remote(recvQ.at[i, yy], recvQ.at[i, yy], sQ.at[i, yy], rQ.at[i, yy], at_t(mate)).wait_recv()
            tot = tot + recvQ[i, yy].astype(F32)
        zs[i] = tot.reshape(16, 8, 128).astype(BF)

        @pl.when(i > 0)
        def _():
            def one(o):
                c, p, copy = z_main(i, o)

                @pl.when(p != b)
                def _():
                    copy.start()

                @pl.when(p == b)
                def _():
                    recvZ[c, b] = zs[i, o]

            loop(16, one)

        @pl.when(i == 0)
        def _():
            loop(32, lambda k: z_rest(lax.rem(b + k, 32)).start(), 1)
            recvZ[0, b] = zs[0, lax.div(b, 2)]

    def turn(i):
        for q in range(8):
            v = XG[q, 0, pl.ds(8 * i, 8)].reshape(128, 128)
            XT[128 * q : 128 * q + 128, pl.ds(pl.multiple_of(128 * i, 128), 128)] = v.T

    def early_grads():
        n = 24
        for u in (1, 2):
            accg[u - 1] = nn(XT[:, : 16 * n], H[u, :n].reshape(16 * n, -1))
        g = jnp.concatenate([XG[q, 1, :n].reshape(16 * n, 128) for q in range(8)], axis=1)
        accd[...] = tn(H[0, :n].reshape(16 * n, -1), g)

    def late_grads(u):
        n = 24
        hv = H[u, n:].reshape(640 - 16 * n, -1)
        if u:
            outg[u - 1] = (accg[u - 1] + nn(XT[:, 16 * n :], hv)).astype(BF)
        else:
            g = jnp.concatenate([XG[q, 1, n:].reshape(640 - 16 * n, 128) for q in range(8)], axis=1)
            outd[...] = (accd[...] + tn(hv, g)).astype(BF)
        grads_out[u].start()

    grads_out = [
        pltpu.make_async_copy(outd, gd_out.at[0], osem.at[0]),
        pltpu.make_async_copy(outg.at[0], gg_out.at[0], osem.at[1]),
        pltpu.make_async_copy(outg.at[1], gu_out.at[0], osem.at[2]),
    ]

    loop(S, turn)
    own(0)
    own(1)
    relay(0)

    def cycle(i):
        @pl.when(i + 2 < S)
        def _():
            own(i + 2)

        @pl.when(i + 1 < S)
        def _():
            relay(i + 1)

        @pl.when(i >= 1)
        def _():
            pair(i - 1)

        @pl.when(i >= 2)
        def _():
            back(i - 2)

        rows(i)

    loop(3, cycle)
    early_grads()
    loop(S, cycle, 3)
    late_grads(1)
    pair(S - 1)
    back(S - 2)
    late_grads(2)
    back(S - 1)
    late_grads(0)

    def wait_z(k):
        p = lax.rem(b + k, 32)
        for c in range(3):
            ref = recvZ.at[c, p]
            remote(ref, ref, sZ.at[c, p], rZ.at[c, p], at_p(p)).wait_recv()

    loop(32, wait_z, 1)
    for dd in range(4):
        z = recvZ[:, 8 * dd : 8 * dd + 8].astype(F32).reshape(PLACES, 128).astype(BF)
        part_rows = nn(tab[...], z).reshape(8, 8, 128).astype(BF)
        sendY[:, :, 128 * dd : 128 * dd + 128] = part_rows

    def y_copy(k):
        q = lax.rem(t + k, 8)
        return remote(sendY.at[q], recvY.at[t], sY.at[q], rY.at[t], at_t(q))

    loop(8, lambda k: y_copy(k).start(), 1)
    recvY[t] = sendY[t]

    loop(8, lambda k: send_a(k).wait_send(), 1)
    for c in range(3):
        loop(32, lambda k, c=c: send_c(c, k).wait_send(), 1)

    def drain(i):
        for k in range(4):
            send_d(i, k, t, mate).wait_send()
        for k in range(1, 4):
            send_d(i, 4 + k, t, mate).wait_send()
            q_send(i, k).wait_send()
        for m in range(6):
            rs_send(i, m).wait_send()
        for m in range(4):
            ag_send(i, m).wait_send()
        p_copy(i).wait_send()

        @pl.when(i > 0)
        def _():
            def one(o):
                c, p, copy = z_main(i, o)

                @pl.when(p != b)
                def _():
                    copy.wait_send()

            loop(16, one)

    loop(S, drain)
    loop(32, lambda k: z_rest(lax.rem(b + k, 32)).wait_send(), 1)

    def wait_y(k):
        q = lax.rem(t + k, 8)
        remote(recvY.at[q], recvY.at[q], sY.at[q], rY.at[q], at_t(q)).wait_recv()

    loop(8, wait_y, 1)
    for dd in range(4):
        for q in range(8):
            at = slice(1024 * dd + 128 * q, 1024 * dd + 128 * q + 128)
            y_out[:, at] = recvY[q, :, 128 * dd : 128 * dd + 128]
    loop(8, lambda k: y_copy(k).wait_send(), 1)
    for c in grads_out:
        c.wait()


def shards(tokens, out_grad, route_probs, expert_ids, slot_index, w_gate, w_up, w_down):
    wg, wu, wd = w_gate[0], w_up[0], w_down[0]
    dl, fl = wg.shape
    vm = pl.BlockSpec(memory_space=pltpu.VMEM)
    hbm = pl.BlockSpec(memory_space=pl.ANY)
    dma = pltpu.SemaphoreType.DMA

    def buf(*shape, dtype=BF):
        return pltpu.VMEM(shape, dtype)

    yv, gg, gu, gd = pl.pallas_call(
        kernel,
        name="expert_back",
        out_shape=(
            jax.ShapeDtypeStruct(tokens.shape, BF),
            jax.ShapeDtypeStruct(w_gate.shape, BF),
            jax.ShapeDtypeStruct(w_up.shape, BF),
            jax.ShapeDtypeStruct(w_down.shape, BF),
        ),
        in_specs=[hbm] * 8,
        out_specs=(vm, hbm, hbm, hbm),
        scratch_shapes=[
            buf(8, 4096), buf(8, 4096), buf(2, 64, dtype=F32),
            buf(2, 64, dtype=jnp.int32), buf(2, 64, dtype=jnp.int32),
            buf(dl, fl), buf(dl, fl), buf(fl, dl), buf(64, PLACES),
            buf(8, 2, 8, 512), buf(8, 2, 8, 512),
            buf(3, 32, 2, 8, 128), buf(3, 32, 2, 8, 128),
            buf(8, 2, 40, 16, 128), buf(dl, 640), buf(3, 40, 16, fl),
            buf(2, S, 3, 16, fl), buf(2, S, 3, 16, fl), buf(2, S, 3, 16, fl), buf(2, S, 3, 16, fl),
            buf(3, 40, 16, fl),
            buf(S, 2, 4, 128, 128), buf(S, 4, 128, 128), buf(S, 4, 128, 128), buf(S, 4, 128, 128),
            buf(S, 16, 8, 128), buf(3, 32, 8, 128), buf(8, 8, 512), buf(8, 8, 512),
            buf(2, dl, fl, dtype=F32), buf(fl, dl, dtype=F32), buf(2, dl, fl), buf(fl, dl),
            dma((5,)), dma((3,)), dma((8,)), dma((8,)), dma((3, 32)), dma((3, 32)),
            dma((S, 8)), dma((S, 8)), dma((S, 6)), dma((S, 6)), dma((S, 4)), dma((S, 4)),
            dma((S,)), dma((S,)), dma((S, 4)), dma((S, 4)), dma((3, 32)), dma((3, 32)),
            dma((8,)), dma((8,)), dma((3,)),
        ],
        compiler_params=pltpu.CompilerParams(
            collective_id=0, has_side_effects=True, vmem_limit_bytes=60 * 1024 * 1024
        ),
    )(tokens, out_grad, route_probs.T, expert_ids.T, slot_index.T, wg, wu, wd)
    return yv, gg, gu, gd


def solution(mesh):
    placed = (
        P(("dp", "expert", "tensor"), None),
        P(("dp", "expert", "tensor"), None),
        P(("dp", "expert"), None),
        P(("dp", "expert"), None),
        P(("dp", "expert"), None),
        P("expert", "dp", "tensor"),
        P("expert", "dp", "tensor"),
        P("expert", "tensor", "dp"),
    )
    return jax.shard_map(
        shards,
        mesh=mesh,
        in_specs=placed,
        out_specs=(
            P(("dp", "expert", "tensor"), None),
            P("expert", "dp", "tensor"),
            P("expert", "dp", "tensor"),
            P("expert", "tensor", "dp"),
        ),
        check_vma=False,
    )
```

time: 199 us -> 177 us (0.89)
  Pallas kernels: 180 us -> 168 us
  matrix products: 10.7 us -> 0 us
  local copies, waits for them, and re-layouts: 3.38 us -> 7.87 us
  other arithmetic: 4.3 us -> 0 us
    pallas_call x1, Pallas kernels: 180 us -> 168 us  [shards(): pl.pallas_call(kernel, name='expert_back', out_shape=(jax.ShapeDtypeStruc...]
    dot_general x3 -> x0, matrix products: 10.7 us -> none  [tn(): lax.dot_general(a, c, (((0,), (0,)), ((), ())), preferred_element_type=F32)]
    unnamed x5 -> x8, local copies, waits for them, and re-layouts: 0.79 us -> 7.87 us
    convert_element_type x3 -> x0, other arithmetic: 2.06 us -> none  [the longest x1 0.72 us: tables(): ((places == at_x[0][:, None]) | (places == at_x[1][:, None])).astype(BF)]
where the time goes in v2:
time: 177 us
  Pallas kernels  168 us (95%)
  local copies, waits for them, and re-layouts  7.87 us (4%)
    pallas_call x1, Pallas kernels, shards(): pl.pallas_call(kernel, name='expert_back', out_shape=(jax.ShapeDtypeStruc...  168 us
    unnamed x8, local copies, waits for them, and re-layouts  7.87 us

profile of v2, /device:TPU:1, one launch (start us, length us, event | category | flops | bytes accessed | tf_op | source)
XLA Modules:
  0.0 176.9 jit_solution(16753156970731911165)
XLA Ops:
  0.6 168.4 %expert_back.1 = (bf16[8,4096]{1,0:T(8,128)(2,1)}, bf16[1,1024,896]{2,1,0:T(8,128)(2,1)}, bf16[1,1024,896]{2,1,0:T(8,128)(2,1)}, bf16[1,896,1024]{2,1,0:T(8,128)(2,1)}) custom-call(bf16[8,4096]{1,0:T(8,128)(2,1)} %tok_hbm.1, bf16[8,4096]{1,0:T(8,128)(2,1)} %og_hbm.1, f32[2,64]{1,0:T(2,128)} %bitcast.9, s32[2,64]{1,0:T(2,128)} %bitcast.10, s32[2,64]{1,0:T(2,128)} %bitcast.11, ...), custom_call_target="tpu_custom_call" | custom-call | tf_op jit(solution)/shard_map/expert_back/pallas_call | solution.py:496
  169.1 1.5 copy.16
  170.5 0.0 copy-start.1
  170.5 3.0 %copy.17 = bf16[1,1024,896]{2,1,0:T(8,128)(2,1)} copy(bf16[1,1024,896]{2,1,0:T(8,128)(2,1)} %get-tuple-element.9) | data formatting | bytes 3670016
  173.5 0.0 copy-done.1
  173.5 0.0 copy-start
  173.5 1.2 copy.18
  174.8 0.9 copy-done
  175.7 1.2 copy.19
Async XLA Ops:
  170.5 3.0 %copy-start.1 = (bf16[1,1024,896]{2,1,0:T(8,128)(2,1)S(1)}, bf16[1,1024,896]{2,1,0:T(8,128)(2,1)}, u32[]{:S(2)}) copy-start(bf16[1,1024,896]{2,1,0:T(8,128)(2,1)} %get-tuple-element.10) | copy-start | bytes 5505028
  173.5 2.2 %copy-start = (bf16[1,896,1024]{2,1,0:T(8,128)(2,1)S(1)}, bf16[1,896,1024]{2,1,0:T(8,128)(2,1)}, u32[]{:S(2)}) copy-start(bf16[1,896,1024]{2,1,0:T(8,128)(2,1)} %get-tuple-element.11) | copy-start | bytes 5505028

commit v3 on v2

--- a/solution.py
+++ b/solution.py
@@ -48,10 +48,10 @@
 def kernel(
     tok_hbm, og_hbm, prob_hbm, id_hbm, slot_hbm, wg_hbm, wu_hbm, wd_hbm,
     y_out, gg_out, gu_out, gd_out,
-    tok, og, prob, ids, slots, wg, wu, wd, tab,
+    tok, og, prob, ids, slots, wg, wu, wd, wgT, wuT, wdT, tab,
     sendA, recvA, sendC, recvC, XG, XT, part, rs1, raw, red, redS, H,
-    rgp, recvP, qs, recvQ, zs, recvZ, sendY, recvY, accg, accd, outg, outd,
-    isem, wsem, sA, rA, sC, rC, sD, rD, sR, rR, sG, rG, sP, rP, sQ, rQ, sZ, rZ, sY, rY, osem,
+    rgp, recvP, qs, recvQ, zs, recvZ, sendY, recvY, accd,
+    isem, wsem, sA, rA, sC, rC, sD, rD, sR, rR, sG, rG, sN, rN, sP, rP, sQ, rQ, sZ, rZ, sY, rY,
 ):
     d, e, t = lax.axis_index("dp"), lax.axis_index("expert"), lax.axis_index("tensor")
     b = d * 8 + e
@@ -65,15 +65,23 @@
     def at_p(p):
         return (lax.div(p, 8), lax.rem(p, 8), t)
 
+    def far_first(n):
+        def swing(m):
+            return lax.div(m + 1, 2) * (1 - 2 * lax.rem(m, 2))
+
+        z = lax.rem(2 * d + lax.div(e, 4) + 4 + swing(lax.div(n, 4)) + 8, 8)
+        x = lax.rem(lax.rem(e, 4) + 2 + swing(lax.rem(n, 4)) + 4, 4)
+        return lax.div(z, 2) * 8 + lax.rem(z, 2) * 4 + x
+
     bar = pltpu.get_barrier_semaphore()
 
     def greet_t(k):
         pl.semaphore_signal(bar, inc=1, device_id=at_t(lax.rem(t + k, 8)), device_id_type=MESH)
 
     def greet_p(k):
-        pl.semaphore_signal(bar, inc=1, device_id=at_p(lax.rem(b + k, 32)), device_id_type=MESH)
-
-    loop(32, greet_p, 1)
+        pl.semaphore_signal(bar, inc=1, device_id=at_p(far_first(k)), device_id_type=MESH)
+
+    loop(31, greet_p)
     loop(8, greet_t, 1)
 
     inputs = [
@@ -134,11 +142,11 @@
                 sendC[c, 8 * dd : 8 * dd + 8, a] = v[cut].reshape(8, 8, 128).astype(BF)
 
     def send_c(c, k):
-        p = lax.rem(b + k, 32)
+        p = far_first(k)
         return remote(sendC.at[c, p], recvC.at[c, b], sC.at[c, p], rC.at[c, b], at_p(p))
 
     for c in range(3):
-        loop(32, lambda k, c=c: send_c(c, k).start(), 1)
+        loop(31, lambda k, c=c: send_c(c, k).start())
         recvC[c, b] = sendC[c, b]
 
     def wait_c(c, p):
@@ -160,9 +168,9 @@
         return recvC[c, p, a].astype(F32)
 
     def start_d(i):
+        for k in (2, 1, 3):
+            send_d(i, k, t, lax.rem(t + 2 * k, 8)).start()
         send_d(i, 0, t, mate).start()
-        for k in range(1, 4):
-            send_d(i, k, t, lax.rem(t + 2 * k, 8)).start()
 
     def relay_d(i):
         for k in (1, 3, 2):
@@ -174,6 +182,20 @@
         for k in range(4):
             wait_d(i, lax.rem(mate + 2 * k, 8))
 
+    for c in weights:
+        c.wait()
+
+    def flip(src, dst):
+        rows, cols = src.shape
+
+        def one(r):
+            at = pl.ds(pl.multiple_of(128 * r, 128), 128)
+            for f in range(cols // 128):
+                dst[128 * f : 128 * f + 128, at] = src[at, 128 * f : 128 * f + 128].T
+
+        loop(rows // 128, one)
+
+    flip(wd, wdT)
     loop(32, lambda p: wait_c(0, p))
 
     def rest(j):
@@ -229,12 +251,9 @@
         xs = rows_of(0, i)
         part[0, tiles] = nn(xs, wg[...]).astype(BF).reshape(8, 16, -1)
         part[1, tiles] = nn(xs, wu[...]).astype(BF).reshape(8, 16, -1)
-        part[2, tiles] = nt(rows_of(1, i), wd[...]).astype(BF).reshape(8, 16, -1)
+        part[2, tiles] = nn(rows_of(1, i), wdT[...]).astype(BF).reshape(8, 16, -1)
         for m in (0, 3, 1, 4):
             rs_send(i, m).start()
-
-    for c in weights:
-        c.wait()
 
     def open_stage(i):
         @pl.when(i < S - 1)
@@ -246,6 +265,8 @@
         forward(i)
 
     loop(S, open_stage)
+    flip(wg, wgT)
+    flip(wu, wuT)
 
     def middle(i):
         rs_wait(i, 0)
@@ -257,39 +278,50 @@
 
     loop(S, middle)
 
+    def ag_ref(i, owner, half=None):
+        return H.at[1:3, i, pl.ds(2 * owner, 2) if half is None else 2 * owner + half]
+
+    def hid_ref(n, owner, half=None):
+        return H.at[0, pl.ds(3 * n, 3 - n), pl.ds(2 * owner, 2) if half is None else 2 * owner + half]
+
+    def ring(ref, i, m, sems):
+        src, dev = {
+            0: (ref(i, d), right), 1: (ref(i, d), left),
+            2: (ref(i, left, 0), right), 3: (ref(i, right, 1), left),
+        }[m]
+        return remote(src, src, sems[0].at[i, m], sems[1].at[i, m], peer(dev))
+
+    def ring_wait(ref, i, m, sems):
+        dst = (ref(i, left), ref(i, right), ref(i, opp, 0), ref(i, opp, 1))[m]
+        remote(dst, dst, sems[0].at[i, m], sems[1].at[i, m], peer(right)).wait_recv()
+
     def ag_send(i, m):
-        src, dev = {
-            0: (H.at[:, pl.ds(tile(i, d, 0), 2)], right),
-            1: (H.at[:, pl.ds(tile(i, d, 0), 2)], left),
-            2: (H.at[:, tile(i, left, 0)], right),
-            3: (H.at[:, tile(i, right, 1)], left),
-        }[m]
-        return remote(src, src, sG.at[i, m], rG.at[i, m], peer(dev))
+        return ring(ag_ref, i, m, (sG, rG))
 
     def ag_wait(i, m):
-        dst = (
-            H.at[:, pl.ds(tile(i, left, 0), 2)],
-            H.at[:, pl.ds(tile(i, right, 0), 2)],
-            H.at[:, tile(i, opp, 0)],
-            H.at[:, tile(i, opp, 1)],
-        )[m]
-        remote(dst, dst, sG.at[i, m], rG.at[i, m], peer(right)).wait_recv()
+        ring_wait(ag_ref, i, m, (sG, rG))
+
+    def hid_send(n, m):
+        return ring(hid_ref, n, m, (sN, rN))
+
+    def hid_wait(n, m):
+        ring_wait(hid_ref, n, m, (sN, rN))
 
     def own(i):
         rs_wait(i, 1)
         rs_wait(i, 4)
         for half, (ra, rb, m) in enumerate(((red, raw, 2), (raw, red, 5))):
             rs_wait(i, m)
-            at = tile(i, d, half)
+            at, to = tile(i, d, half), 2 * d + half
             gate, up, grad = (
                 part[u, at].astype(F32) + ra[0, i, u].astype(F32) + rb[1, i, u].astype(F32)
                 for u in range(3)
             )
             s = jax.nn.sigmoid(gate)
             silu = gate * s
-            H[0, at] = (silu * up).astype(BF)
-            H[1, at] = (grad * up * s * (1.0 + gate * (1.0 - s))).astype(BF)
-            H[2, at] = (grad * silu).astype(BF)
+            H[0, i, to] = (silu * up).astype(BF)
+            H[1, i, to] = (grad * up * s * (1.0 + gate * (1.0 - s))).astype(BF)
+            H[2, i, to] = (grad * silu).astype(BF)
         ag_send(i, 0).start()
         ag_send(i, 1).start()
 
@@ -307,12 +339,12 @@
         return remote(qs.at[i, yy], recvQ.at[i, y], sQ.at[i, yy], rQ.at[i, y], at_t(2 * yy + core))
 
     def hid(u, i):
-        return H[u, pl.ds(8 * i, 8)].reshape(128, -1)
+        return H[u, i].reshape(128, -1)
 
     def rows(i):
         ag_wait(i, 2)
         ag_wait(i, 3)
-        rg = nt(hid(1, i), wg[...]) + nt(hid(2, i), wu[...])
+        rg = nn(hid(1, i), wgT[...]) + nn(hid(2, i), wuT[...])
         for q in range(8):
             rgp[i, q % 2, q // 2] = rg[:, 128 * q : 128 * q + 128].astype(BF)
         p_copy(i).start()
@@ -355,7 +387,7 @@
 
         @pl.when(i == 0)
         def _():
-            loop(32, lambda k: z_rest(lax.rem(b + k, 32)).start(), 1)
+            loop(31, lambda k: z_rest(far_first(k)).start())
             recvZ[0, b] = zs[0, lax.div(b, 2)]
 
     def turn(i):
@@ -363,28 +395,14 @@
             v = XG[q, 0, pl.ds(8 * i, 8)].reshape(128, 128)
             XT[128 * q : 128 * q + 128, pl.ds(pl.multiple_of(128 * i, 128), 128)] = v.T
 
-    def early_grads():
-        n = 24
-        for u in (1, 2):
-            accg[u - 1] = nn(XT[:, : 16 * n], H[u, :n].reshape(16 * n, -1))
-        g = jnp.concatenate([XG[q, 1, :n].reshape(16 * n, 128) for q in range(8)], axis=1)
-        accd[...] = tn(H[0, :n].reshape(16 * n, -1), g)
-
-    def late_grads(u):
-        n = 24
-        hv = H[u, n:].reshape(640 - 16 * n, -1)
-        if u:
-            outg[u - 1] = (accg[u - 1] + nn(XT[:, 16 * n :], hv)).astype(BF)
-        else:
-            g = jnp.concatenate([XG[q, 1, n:].reshape(640 - 16 * n, 128) for q in range(8)], axis=1)
-            outd[...] = (accd[...] + tn(hv, g)).astype(BF)
-        grads_out[u].start()
-
-    grads_out = [
-        pltpu.make_async_copy(outd, gd_out.at[0], osem.at[0]),
-        pltpu.make_async_copy(outg.at[0], gg_out.at[0], osem.at[1]),
-        pltpu.make_async_copy(outg.at[1], gu_out.at[0], osem.at[2]),
-    ]
+    def model_grad(u, out):
+        out[0] = nn(XT[...], H[u].reshape(640, -1)).astype(BF)
+
+    def down_part(lo, hi):
+        g = jnp.concatenate(
+            [XG[q, 1, 8 * lo : 8 * hi].reshape(128 * (hi - lo), 128) for q in range(8)], axis=1
+        )
+        return tn(H[0, lo:hi].reshape(128 * (hi - lo), -1), g)
 
     loop(S, turn)
     own(0)
@@ -400,6 +418,11 @@
         def _():
             relay(i + 1)
 
+        @pl.when(i == S - 2)
+        def _():
+            for m in (0, 1):
+                hid_send(0, m).start()
+
         @pl.when(i >= 1)
         def _():
             pair(i - 1)
@@ -410,15 +433,22 @@
 
         rows(i)
 
-    loop(3, cycle)
-    early_grads()
-    loop(S, cycle, 3)
-    late_grads(1)
+    loop(S, cycle)
     pair(S - 1)
     back(S - 2)
-    late_grads(2)
+    model_grad(1, gg_out)
     back(S - 1)
-    late_grads(0)
+    for m in (0, 1):
+        hid_send(1, m).start()
+
+    def hid_relay(n):
+        for m in (0, 1):
+            hid_wait(n, m)
+            hid_send(n, m + 2).start()
+
+    hid_relay(0)
+    model_grad(2, gu_out)
+    hid_relay(1)
 
     def wait_z(k):
         p = lax.rem(b + k, 32)
@@ -438,10 +468,13 @@
 
     loop(8, lambda k: y_copy(k).start(), 1)
     recvY[t] = sendY[t]
+    for m in (2, 3):
+        hid_wait(0, m)
+    accd[...] = down_part(0, 3)
 
     loop(8, lambda k: send_a(k).wait_send(), 1)
     for c in range(3):
-        loop(32, lambda k, c=c: send_c(c, k).wait_send(), 1)
+        loop(31, lambda k, c=c: send_c(c, k).wait_send())
 
     def drain(i):
         for k in range(4):
@@ -467,7 +500,7 @@
             loop(16, one)
 
     loop(S, drain)
-    loop(32, lambda k: z_rest(lax.rem(b + k, 32)).wait_send(), 1)
+    loop(31, lambda k: z_rest(far_first(k)).wait_send())
 
     def wait_y(k):
         q = lax.rem(t + k, 8)
@@ -479,8 +512,12 @@
             at = slice(1024 * dd + 128 * q, 1024 * dd + 128 * q + 128)
             y_out[:, at] = recvY[q, :, 128 * dd : 128 * dd + 128]
     loop(8, lambda k: y_copy(k).wait_send(), 1)
-    for c in grads_out:
-        c.wait()
+    for m in (2, 3):
+        hid_wait(1, m)
+    gd_out[0] = (accd[...] + down_part(3, S)).astype(BF)
+    for n in (0, 1):
+        for m in range(4):
+            hid_send(n, m).wait_send()
 
 
 def shards(tokens, out_grad, route_probs, expert_ids, slot_index, w_gate, w_up, w_down):
@@ -503,26 +540,26 @@
             jax.ShapeDtypeStruct(w_down.shape, BF),
         ),
         in_specs=[hbm] * 8,
-        out_specs=(vm, hbm, hbm, hbm),
+        out_specs=(vm, vm, vm, vm),
         scratch_shapes=[
             buf(8, 4096), buf(8, 4096), buf(2, 64, dtype=F32),
             buf(2, 64, dtype=jnp.int32), buf(2, 64, dtype=jnp.int32),
-            buf(dl, fl), buf(dl, fl), buf(fl, dl), buf(64, PLACES),
+            buf(dl, fl), buf(dl, fl), buf(fl, dl), buf(fl, dl), buf(fl, dl), buf(dl, fl), buf(64, PLACES),
             buf(8, 2, 8, 512), buf(8, 2, 8, 512),
             buf(3, 32, 2, 8, 128), buf(3, 32, 2, 8, 128),
             buf(8, 2, 40, 16, 128), buf(dl, 640), buf(3, 40, 16, fl),
             buf(2, S, 3, 16, fl), buf(2, S, 3, 16, fl), buf(2, S, 3, 16, fl), buf(2, S, 3, 16, fl),
-            buf(3, 40, 16, fl),
+            buf(3, S, 8, 16, fl),
             buf(S, 2, 4, 128, 128), buf(S, 4, 128, 128), buf(S, 4, 128, 128), buf(S, 4, 128, 128),
             buf(S, 16, 8, 128), buf(3, 32, 8, 128), buf(8, 8, 512), buf(8, 8, 512),
-            buf(2, dl, fl, dtype=F32), buf(fl, dl, dtype=F32), buf(2, dl, fl), buf(fl, dl),
+            buf(fl, dl, dtype=F32),
             dma((5,)), dma((3,)), dma((8,)), dma((8,)), dma((3, 32)), dma((3, 32)),
             dma((S, 8)), dma((S, 8)), dma((S, 6)), dma((S, 6)), dma((S, 4)), dma((S, 4)),
-            dma((S,)), dma((S,)), dma((S, 4)), dma((S, 4)), dma((3, 32)), dma((3, 32)),
-            dma((8,)), dma((8,)), dma((3,)),
+            dma((2, 4)), dma((2, 4)), dma((S,)), dma((S,)), dma((S, 4)), dma((S, 4)), dma((3, 32)), dma((3, 32)),
+            dma((8,)), dma((8,)),
         ],
         compiler_params=pltpu.CompilerParams(
-            collective_id=0, has_side_effects=True, vmem_limit_bytes=60 * 1024 * 1024
+            collective_id=0, has_side_effects=True, vmem_limit_bytes=48 * 1024 * 1024
         ),
     )(tokens, out_grad, route_probs.T, expert_ids.T, slot_index.T, wg, wu, wd)
     return yv, gg, gu, gd

time: 177 us -> 169 us (0.955)
  Pallas kernels: 168 us -> 160 us
    pallas_call x1, Pallas kernels: 168 us -> 160 us  [shards(): pl.pallas_call(kernel, name='expert_back', out_shape=(jax.ShapeDtypeStruc...]
    unnamed x8 -> x14, local copies, waits for them, and re-layouts: 7.87 us -> 8.02 us
where the time goes in v3:
time: 169 us
  Pallas kernels  160 us (95%)
  local copies, waits for them, and re-layouts  8.02 us (5%)
    pallas_call x1, Pallas kernels, shards(): pl.pallas_call(kernel, name='expert_back', out_shape=(jax.ShapeDtypeStruc...  160 us
    unnamed x14, local copies, waits for them, and re-layouts  8.02 us

profile of v3, /device:TPU:1, one launch (start us, length us, event | category | flops | bytes accessed | tf_op | source)
XLA Modules:
  0.0 168.7 jit_solution(14271473051754536717)
XLA Ops:
  0.6 0.0 copy-start
  0.6 0.8 copy-done
  1.5 0.0 copy-start.1
  1.5 0.8 copy-done.1
  2.3 0.0 copy-start.2
  2.3 0.7 copy-done.2
  3.0 0.0 copy-start.3
  3.0 0.7 copy-done.3
  3.7 0.0 copy-start.4
  3.7 0.7 copy-done.4
  4.4 160.1 %expert_back.1 = (bf16[8,4096]{1,0:T(8,128)(2,1)S(1)}, bf16[1,1024,896]{2,1,0:T(8,128)(2,1)S(1)}, bf16[1,1024,896]{2,1,0:T(8,128)(2,1)S(1)}, bf16[1,896,1024]{2,1,0:T(8,128)(2,1)S(1)}) custom-call(bf16[8,4096]{1,0:T(8,128)(2,1)S(1)} %copy-done, bf16[8,4096]{1,0:T(8,128)(2,1)S(1)} %copy-done.1, f32[2,64]{1,0:T(2,128)S(1)} %bitcast.6, s32[2,64]{1,0:T(2,128)S(1)} %bitcast.7, ...), custom_call_target="tpu_custom_call" | custom-call | tf_op jit(solution)/shard_map/expert_back/pallas_call | solution.py:533
  164.4 0.6 copy.16
  165.1 1.2 copy.17
  166.3 1.2 copy.18
  167.5 1.2 copy.19
Async XLA Ops:
  0.6 0.8 copy-start
  1.5 0.8 copy-start.1
  2.3 0.7 copy-start.2
  3.0 0.7 copy-start.3
  3.7 0.7 copy-start.4

commit v4 on v3

--- a/solution.py
+++ b/solution.py
@@ -49,9 +49,9 @@
     tok_hbm, og_hbm, prob_hbm, id_hbm, slot_hbm, wg_hbm, wu_hbm, wd_hbm,
     y_out, gg_out, gu_out, gd_out,
     tok, og, prob, ids, slots, wg, wu, wd, wgT, wuT, wdT, tab,
-    sendA, recvA, sendC, recvC, XG, XT, part, rs1, raw, red, redS, H,
+    sendA, recvA, sendR, recvR, sendC, recvC, XG, XT, part, rs1, raw, red, redS, H,
     rgp, recvP, qs, recvQ, zs, recvZ, sendY, recvY, accd,
-    isem, wsem, sA, rA, sC, rC, sD, rD, sR, rR, sG, rG, sN, rN, sP, rP, sQ, rQ, sZ, rZ, sY, rY,
+    isem, wsem, sA, rA, sL, rL, sC, rC, sD, rD, sR, rR, sG, rG, sN, rN, sP, rP, sQ, rQ, sZ, rZ, sY, rY,
 ):
     d, e, t = lax.axis_index("dp"), lax.axis_index("expert"), lax.axis_index("tensor")
     b = d * 8 + e
@@ -104,17 +104,18 @@
             sendA[q, 0, :, 128 * dd : 128 * dd + 128] = tok[:, at]
             sendA[q, 1, :, 128 * dd : 128 * dd + 128] = og[:, at]
     slot, owner = slots[...], ids[...] * 8
-    place = jnp.where(
-        slot >= 16,
-        owner + 4 * lax.rem(e, 2) + slot - 16,
-        jnp.where(slot < 8, 64 + owner + slot, 120 + owner + slot),
-    )
-    place = jnp.where(slot < CAP, place, -1)
+    past = slot >= 16
+    low = jnp.where(slot < 8, 64 + owner + slot, 120 + owner + slot)
+
+    def places(extra):
+        return jnp.where(slot < CAP, jnp.where(past, owner + slot - 16 + extra, low), -1)
+
+    place_x, place_g, place_z = places(0), places(4), places(4 * lax.rem(e, 2))
     by_place = lax.broadcasted_iota(jnp.int32, (PLACES, 64), 0)
-    t0, t1 = ((by_place == place[k : k + 1]).astype(F32) for k in range(2))
-    tx, t0, t1 = (t0 + t1).astype(BF), t0.astype(BF), t1.astype(BF)
+    tx = sum((by_place == place_x[k : k + 1]).astype(F32) for k in range(2)).astype(BF)
+    t0, t1 = ((by_place == place_g[k : k + 1]).astype(BF) for k in range(2))
     by_token = lax.broadcasted_iota(jnp.int32, (64, PLACES), 1)
-    tab[...] = sum((by_token == column(place[k : k + 1])).astype(F32) for k in range(2)).astype(BF)
+    tab[...] = sum((by_token == column(place_z[k : k + 1])).astype(F32) for k in range(2)).astype(BF)
     p0, p1 = (column(prob[k : k + 1]) for k in range(2))
     pl.semaphore_wait(bar, 38)
 
@@ -135,52 +136,67 @@
     ry = recvA[:, 1].astype(F32).reshape(64, 512)
     xb = nn(tx, rx)
     gb = nn(t0, (p0 * ry).astype(BF)) + nn(t1, (p1 * ry).astype(BF))
-    for c in range(3):
-        for dd in range(4):
-            cut = slice(64 * c, 64 * c + 64), slice(128 * dd, 128 * dd + 128)
+    for dd in range(4):
+        cols, to = slice(128 * dd, 128 * dd + 128), slice(8 * dd, 8 * dd + 8)
+        sendR[to] = (xb[:64, cols] + gb[:64, cols]).reshape(8, 8, 128).astype(BF)
+        for c in range(2):
             for a, v in enumerate((xb, gb)):
-                sendC[c, 8 * dd : 8 * dd + 8, a] = v[cut].reshape(8, 8, 128).astype(BF)
+                sendC[c, to, a] = v[64 * c + 64 : 64 * c + 128, cols].reshape(8, 8, 128).astype(BF)
+
+    def send_l(k):
+        p = far_first(k)
+        return remote(sendR.at[p], recvR.at[b], sL.at[p], rL.at[b], at_p(p))
 
     def send_c(c, k):
         p = far_first(k)
         return remote(sendC.at[c, p], recvC.at[c, b], sC.at[c, p], rC.at[c, b], at_p(p))
 
-    for c in range(3):
+    loop(31, lambda k: send_l(k).start())
+    recvR[b] = sendR[b]
+    for c in range(2):
         loop(31, lambda k, c=c: send_c(c, k).start())
         recvC[c, b] = sendC[c, b]
 
+    def wait_l(p):
+        @pl.when(p != b)
+        def _():
+            remote(recvR.at[p], recvR.at[p], sL.at[p], rL.at[p], at_p(p)).wait_recv()
+
     def wait_c(c, p):
         @pl.when(p != b)
         def _():
             ref = recvC.at[c, p]
             remote(ref, ref, sC.at[c, p], rC.at[c, p], at_p(p)).wait_recv()
 
-    def piece(src, i):
-        return XG.at[src, :, pl.ds(8 * i, 8)]
-
-    def send_d(i, slot, src, dst):
-        return remote(piece(src, i), piece(src, i), sD.at[i, slot], rD.at[i, src], at_t(dst))
-
-    def wait_d(i, src):
-        remote(piece(src, i), piece(src, i), sD.at[i, 0], rD.at[i, src], at_t(mate)).wait_recv()
+    def piece(src, a, i):
+        return XG.at[src, a, pl.ds(8 * i, 8)]
+
+    def send_d(i, a, slot, src, dst):
+        ref = piece(src, a, i)
+        return remote(ref, ref, sD.at[i, a, slot], rD.at[i, a, src], at_t(dst))
+
+    def wait_d(i, a, src):
+        ref = piece(src, a, i)
+        remote(ref, ref, sD.at[i, a, 0], rD.at[i, a, src], at_t(mate)).wait_recv()
 
     def octet(c, p, a):
         return recvC[c, p, a].astype(F32)
 
     def start_d(i):
-        for k in (2, 1, 3):
-            send_d(i, k, t, lax.rem(t + 2 * k, 8)).start()
-        send_d(i, 0, t, mate).start()
-
-    def relay_d(i):
+        for a in range(2):
+            for k in (2, 1, 3):
+                send_d(i, a, k, t, lax.rem(t + 2 * k, 8)).start()
+            send_d(i, a, 0, t, mate).start()
+
+    def relay_d(i, a):
         for k in (1, 3, 2):
             q = lax.rem(t + 2 * k, 8)
-            wait_d(i, q)
-            send_d(i, 4 + k, q, mate).start()
-
-    def arrive_d(i):
+            wait_d(i, a, q)
+            send_d(i, a, 4 + k, q, mate).start()
+
+    def arrive_d(i, a):
         for k in range(4):
-            wait_d(i, lax.rem(mate + 2 * k, 8))
+            wait_d(i, a, lax.rem(mate + 2 * k, 8))
 
     for c in weights:
         c.wait()
@@ -196,19 +212,18 @@
         loop(rows // 128, one)
 
     flip(wd, wdT)
-    loop(32, lambda p: wait_c(0, p))
+    loop(32, wait_l)
 
     def rest(j):
+        four = [recvR[4 * j + q].astype(F32) for q in range(4)]
         for a in range(2):
-            lo = octet(0, 4 * j, a) + octet(0, 4 * j + 1, a)
-            hi = octet(0, 4 * j + 2, a) + octet(0, 4 * j + 3, a)
-            XG[t, a, j] = jnp.concatenate([lo, hi], axis=0).astype(BF)
+            XG[t, a, j] = jnp.concatenate([v[4 * a : 4 * a + 4] for v in four], axis=0).astype(BF)
 
     loop(8, rest)
     start_d(0)
 
     def prep(i):
-        c, first = lax.div(i + 1, 2), 16 * lax.rem(i + 1, 2)
+        c, first = lax.div(i - 1, 2), 16 * lax.rem(i + 1, 2)
 
         def one(j):
             p = first + 2 * j
@@ -227,20 +242,27 @@
     def peer(dd):
         return (dd, e, t)
 
-    def rs_send(i, m):
+    UNITS = (slice(0, 2), slice(2, 3), slice(0, 3))
+
+    def rs_send(i, m, w=2):
+        u = UNITS[w]
         src, dst, dev = {
-            0: (part.at[:, tile(i, opp, 0)], rs1.at[0, i], right),
-            1: (part.at[:, tile(i, right, 1)], raw.at[0, i], right),
+            0: (part.at[u, tile(i, opp, 0)], rs1.at[0, i, u], right),
+            1: (part.at[u, tile(i, right, 1)], raw.at[0, i, u], right),
             2: (redS.at[0, i], red.at[0, i], right),
-            3: (part.at[:, tile(i, opp, 1)], rs1.at[1, i], left),
-            4: (part.at[:, tile(i, left, 0)], raw.at[1, i], left),
+            3: (part.at[u, tile(i, opp, 1)], rs1.at[1, i, u], left),
+            4: (part.at[u, tile(i, left, 0)], raw.at[1, i, u], left),
             5: (redS.at[1, i], red.at[1, i], left),
         }[m]
-        return remote(src, dst, sR.at[i, m], rR.at[i, m], peer(dev))
+        return remote(src, dst, sR.at[i, m, w % 2], rR.at[i, m, w % 2], peer(dev))
 
     def rs_wait(i, m):
-        dst = (rs1, raw, red)[m % 3].at[m // 3, i]
-        remote(dst, dst, sR.at[i, m], rR.at[i, m], peer(right)).wait_recv()
+        for w in (2,) if m % 3 == 2 else (0, 1):
+            dst = (rs1, raw, red)[m % 3].at[m // 3, i, UNITS[w]]
+            remote(dst, dst, sR.at[i, m, w % 2], rR.at[i, m, w % 2], peer(right)).wait_recv()
+
+    def rs_sends(i):
+        return [rs_send(i, m, w) for m in (0, 1, 3, 4) for w in (0, 1)] + [rs_send(i, 2), rs_send(i, 5)]
 
     def rows_of(a, i):
         tiles = pl.ds(8 * i, 8)
@@ -248,20 +270,24 @@
 
     def forward(i):
         tiles = pl.ds(8 * i, 8)
+        relay_d(i, 0)
+        arrive_d(i, 0)
         xs = rows_of(0, i)
         part[0, tiles] = nn(xs, wg[...]).astype(BF).reshape(8, 16, -1)
         part[1, tiles] = nn(xs, wu[...]).astype(BF).reshape(8, 16, -1)
+        for m in (0, 3, 1, 4):
+            rs_send(i, m, 0).start()
+        relay_d(i, 1)
+        arrive_d(i, 1)
         part[2, tiles] = nn(rows_of(1, i), wdT[...]).astype(BF).reshape(8, 16, -1)
         for m in (0, 3, 1, 4):
-            rs_send(i, m).start()
+            rs_send(i, m, 1).start()
 
     def open_stage(i):
         @pl.when(i < S - 1)
         def _():
             prep(i + 1)
 
-        relay_d(i)
-        arrive_d(i)
         forward(i)
 
     loop(S, open_stage)
@@ -278,11 +304,13 @@
 
     loop(S, middle)
 
+    HID = (slice(0, 3), slice(3, 4), slice(4, 5))
+
     def ag_ref(i, owner, half=None):
         return H.at[1:3, i, pl.ds(2 * owner, 2) if half is None else 2 * owner + half]
 
     def hid_ref(n, owner, half=None):
-        return H.at[0, pl.ds(3 * n, 3 - n), pl.ds(2 * owner, 2) if half is None else 2 * owner + half]
+        return H.at[0, HID[n], pl.ds(2 * owner, 2) if half is None else 2 * owner + half]
 
     def ring(ref, i, m, sems):
         src, dev = {
@@ -407,12 +435,13 @@
     loop(S, turn)
     own(0)
     own(1)
+    own(2)
     relay(0)
 
     def cycle(i):
-        @pl.when(i + 2 < S)
-        def _():
-            own(i + 2)
+        @pl.when(i + 3 < S)
+        def _():
+            own(i + 3)
 
         @pl.when(i + 1 < S)
         def _():
@@ -438,8 +467,9 @@
     back(S - 2)
     model_grad(1, gg_out)
     back(S - 1)
-    for m in (0, 1):
-        hid_send(1, m).start()
+    for n in (1, 2):
+        for m in (0, 1):
+            hid_send(n, m).start()
 
     def hid_relay(n):
         for m in (0, 1):
@@ -449,6 +479,7 @@
     hid_relay(0)
     model_grad(2, gu_out)
     hid_relay(1)
+    hid_relay(2)
 
     def wait_z(k):
         p = lax.rem(b + k, 32)
@@ -468,22 +499,24 @@
 
     loop(8, lambda k: y_copy(k).start(), 1)
     recvY[t] = sendY[t]
-    for m in (2, 3):
-        hid_wait(0, m)
-    accd[...] = down_part(0, 3)
+    for n in (0, 1):
+        for m in (2, 3):
+            hid_wait(n, m)
+    accd[...] = down_part(0, 4)
 
     loop(8, lambda k: send_a(k).wait_send(), 1)
-    for c in range(3):
+    loop(31, lambda k: send_l(k).wait_send())
+    for c in range(2):
         loop(31, lambda k, c=c: send_c(c, k).wait_send())
 
     def drain(i):
-        for k in range(4):
-            send_d(i, k, t, mate).wait_send()
+        for a in range(2):
+            for k in (0, 1, 2, 3, 5, 6, 7):
+                send_d(i, a, k, t, mate).wait_send()
         for k in range(1, 4):
-            send_d(i, 4 + k, t, mate).wait_send()
             q_send(i, k).wait_send()
-        for m in range(6):
-            rs_send(i, m).wait_send()
+        for c in rs_sends(i):
+            c.wait_send()
         for m in range(4):
             ag_send(i, m).wait_send()
         p_copy(i).wait_send()
@@ -513,11 +546,20 @@
             y_out[:, at] = recvY[q, :, 128 * dd : 128 * dd + 128]
     loop(8, lambda k: y_copy(k).wait_send(), 1)
     for m in (2, 3):
-        hid_wait(1, m)
-    gd_out[0] = (accd[...] + down_part(3, S)).astype(BF)
-    for n in (0, 1):
+        hid_wait(2, m)
+    gd_out[0] = (accd[...] + down_part(4, S)).astype(BF)
+    for n in range(3):
         for m in range(4):
             hid_send(n, m).wait_send()
+
+
+def put_out(*refs):
+    sems = refs[8]
+    copies = [pltpu.make_async_copy(refs[n], refs[4 + n], sems.at[n]) for n in range(4)]
+    for c in copies:
+        c.start()
+    for c in copies:
+        c.wait()
 
 
 def shards(tokens, out_grad, route_probs, expert_ids, slot_index, w_gate, w_up, w_down):
@@ -546,23 +588,34 @@
             buf(2, 64, dtype=jnp.int32), buf(2, 64, dtype=jnp.int32),
             buf(dl, fl), buf(dl, fl), buf(fl, dl), buf(fl, dl), buf(fl, dl), buf(dl, fl), buf(64, PLACES),
             buf(8, 2, 8, 512), buf(8, 2, 8, 512),
-            buf(3, 32, 2, 8, 128), buf(3, 32, 2, 8, 128),
+            buf(32, 8, 128), buf(32, 8, 128), buf(2, 32, 2, 8, 128), buf(2, 32, 2, 8, 128),
             buf(8, 2, 40, 16, 128), buf(dl, 640), buf(3, 40, 16, fl),
             buf(2, S, 3, 16, fl), buf(2, S, 3, 16, fl), buf(2, S, 3, 16, fl), buf(2, S, 3, 16, fl),
             buf(3, S, 8, 16, fl),
             buf(S, 2, 4, 128, 128), buf(S, 4, 128, 128), buf(S, 4, 128, 128), buf(S, 4, 128, 128),
             buf(S, 16, 8, 128), buf(3, 32, 8, 128), buf(8, 8, 512), buf(8, 8, 512),
             buf(fl, dl, dtype=F32),
-            dma((5,)), dma((3,)), dma((8,)), dma((8,)), dma((3, 32)), dma((3, 32)),
-            dma((S, 8)), dma((S, 8)), dma((S, 6)), dma((S, 6)), dma((S, 4)), dma((S, 4)),
-            dma((2, 4)), dma((2, 4)), dma((S,)), dma((S,)), dma((S, 4)), dma((S, 4)), dma((3, 32)), dma((3, 32)),
+            dma((5,)), dma((3,)), dma((8,)), dma((8,)), dma((32,)), dma((32,)), dma((2, 32)), dma((2, 32)),
+            dma((S, 2, 8)), dma((S, 2, 8)), dma((S, 6, 2)), dma((S, 6, 2)), dma((S, 4)), dma((S, 4)),
+            dma((3, 4)), dma((3, 4)), dma((S,)), dma((S,)), dma((S, 4)), dma((S, 4)), dma((3, 32)), dma((3, 32)),
             dma((8,)), dma((8,)),
         ],
         compiler_params=pltpu.CompilerParams(
             collective_id=0, has_side_effects=True, vmem_limit_bytes=48 * 1024 * 1024
         ),
-    )(tokens, out_grad, route_probs.T, expert_ids.T, slot_index.T, wg, wu, wd)
-    return yv, gg, gu, gd
+    )(*(
+        pltpu.with_memory_space_constraint(v, pltpu.HBM)
+        for v in (tokens, out_grad, route_probs.T, expert_ids.T, slot_index.T, wg, wu, wd)
+    ))
+    return pl.pallas_call(
+        put_out,
+        name="put_out",
+        out_shape=tuple(jax.ShapeDtypeStruct(v.shape, v.dtype) for v in (yv, gg, gu, gd)),
+        in_specs=[hbm] * 4,
+        out_specs=(hbm,) * 4,
+        scratch_shapes=[dma((4,))],
+        compiler_params=pltpu.CompilerParams(vmem_limit_bytes=1024 * 1024),
+    )(yv, gg, gu, gd)
 
 
 def solution(mesh):

time: 169 us -> 164 us (0.970)
  local copies, waits for them, and re-layouts: 8.02 us -> 0 us
  Pallas kernels: 160 us -> 162 us
    unnamed x14 -> x0, local copies, waits for them, and re-layouts: 8.02 us -> none
    pallas_call x0 -> x1, Pallas kernels: none -> 2.49 us  [shards(): pl.pallas_call(put_out, name='put_out', out_shape=tuple((jax.ShapeDtypeSt...]
where the time goes in v4:
time: 164 us; the launch traced here: 163 us
  Pallas kernels  162 us (99%)
    pallas_call x1, Pallas kernels, shards(): pl.pallas_call(kernel, name='expert_back', out_shape=(jax.ShapeDtypeStruc...  160 us

profile of v4, /device:TPU:1, one launch (start us, length us, event | category | flops | bytes accessed | tf_op | source)
XLA Modules:
  0.0 162.8 jit_solution(10337406953266013114)
XLA Ops:
  0.6 159.7 %expert_back.1 = (bf16[8,4096]{1,0:T(8,128)(2,1)S(1)}, bf16[1,1024,896]{2,1,0:T(8,128)(2,1)S(1)}, bf16[1,1024,896]{2,1,0:T(8,128)(2,1)S(1)}, bf16[1,896,1024]{2,1,0:T(8,128)(2,1)S(1)}) custom-call(bf16[8,4096]{1,0:T(8,128)(2,1)} %tok_hbm.1, bf16[8,4096]{1,0:T(8,128)(2,1)} %og_hbm.1, f32[2,64]{1,0:T(2,128)} %bitcast.9, s32[2,64]{1,0:T(2,128)} %bitcast.10, ...), custom_call_target="tpu_custom_call" | custom-call | tf_op jit(solution)/shard_map/expert_back/pallas_call | solution.py:575
  160.3 2.5 %put_out.1 = (bf16[8,4096]{1,0:T(8,128)(2,1)}, bf16[1,1024,896]{2,1,0:T(8,128)(2,1)}, bf16[1,1024,896]{2,1,0:T(8,128)(2,1)}, bf16[1,896,1024]{2,1,0:T(8,128)(2,1)}) custom-call(bf16[8,4096]{1,0:T(8,128)(2,1)S(1)} %get-tuple-element.8.refs_0_, bf16[1,1024,896]{2,1,0:T(8,128)(2,1)S(1)} %get-tuple-element.9.refs_1_, ...), custom_call_target="tpu_custom_call" | custom-call | tf_op jit(solution)/shard_map/put_out/pallas_call | solution.py:610

commit v5 on v4

--- a/solution.py
+++ b/solution.py
@@ -51,7 +51,7 @@
     tok, og, prob, ids, slots, wg, wu, wd, wgT, wuT, wdT, tab,
     sendA, recvA, sendR, recvR, sendC, recvC, XG, XT, part, rs1, raw, red, redS, H,
     rgp, recvP, qs, recvQ, zs, recvZ, sendY, recvY, accd,
-    isem, wsem, sA, rA, sL, rL, sC, rC, sD, rD, sR, rR, sG, rG, sN, rN, sP, rP, sQ, rQ, sZ, rZ, sY, rY,
+    isem, wsem, one, rC, rD, rR, rG, rN, rP, rQ,
 ):
     d, e, t = lax.axis_index("dp"), lax.axis_index("expert"), lax.axis_index("tensor")
     b = d * 8 + e
@@ -59,8 +59,18 @@
     mate = t + 1 - 2 * core
     right, left, opp = lax.rem(d + 1, 4), lax.rem(d + 3, 4), lax.rem(d + 2, 4)
 
+    sA, rA, sL, rL, sC, sD, sR1, sRaw, sRed, sG, sN, sP, sQ, sZ, rZ, sY, rY = (
+        one.at[n] for n in range(17)
+    )
+
     def at_t(tt):
         return (d, e, tt)
+
+    def got(ref, sem):
+        remote(ref, ref, sem, sem, (d, e, mate)).wait_recv()
+
+    def sent(ref, sem):
+        remote(ref, ref, sem, sem, (d, e, mate)).wait_send()
 
     def at_p(p):
         return (lax.div(p, 8), lax.rem(p, 8), t)
@@ -121,16 +131,11 @@
 
     def send_a(k):
         q = lax.rem(t + k, 8)
-        return remote(sendA.at[q], recvA.at[t], sA.at[q], rA.at[t], at_t(q))
-
-    loop(8, lambda k: send_a(k).start(), 1)
+        remote(sendA.at[q], recvA.at[t], sA, rA, at_t(q)).start()
+
+    loop(8, send_a, 1)
     recvA[t] = sendA[t]
-
-    def wait_a(k):
-        q = lax.rem(t + k, 8)
-        remote(recvA.at[q], recvA.at[q], sA.at[q], rA.at[q], at_t(q)).wait_recv()
-
-    loop(8, wait_a, 1)
+    got(recvA.at[0:7], rA)
 
     rx = recvA[:, 0].astype(F32).reshape(64, 512).astype(BF)
     ry = recvA[:, 1].astype(F32).reshape(64, 512)
@@ -145,39 +150,26 @@
 
     def send_l(k):
         p = far_first(k)
-        return remote(sendR.at[p], recvR.at[b], sL.at[p], rL.at[b], at_p(p))
-
-    def send_c(c, k):
-        p = far_first(k)
-        return remote(sendC.at[c, p], recvC.at[c, b], sC.at[c, p], rC.at[c, b], at_p(p))
-
-    loop(31, lambda k: send_l(k).start())
-    recvR[b] = sendR[b]
+        remote(sendR.at[p], recvR.at[b], sL, rL, at_p(p)).start()
+
+    loop(31, send_l)
+    pltpu.make_async_copy(sendR.at[b], recvR.at[b], rL).start()
     for c in range(2):
-        loop(31, lambda k, c=c: send_c(c, k).start())
-        recvC[c, b] = sendC[c, b]
-
-    def wait_l(p):
-        @pl.when(p != b)
-        def _():
-            remote(recvR.at[p], recvR.at[p], sL.at[p], rL.at[p], at_p(p)).wait_recv()
-
-    def wait_c(c, p):
-        @pl.when(p != b)
-        def _():
-            ref = recvC.at[c, p]
-            remote(ref, ref, sC.at[c, p], rC.at[c, p], at_p(p)).wait_recv()
+        sem = rC.at[c, lax.div(d, 2)]
+
+        def send_c(k, c=c, sem=sem):
+            p = far_first(k)
+            remote(sendC.at[c, p], recvC.at[c, b], sC, sem, at_p(p)).start()
+
+        loop(31, send_c)
+        pltpu.make_async_copy(sendC.at[c, b], recvC.at[c, b], sem).start()
 
     def piece(src, a, i):
         return XG.at[src, a, pl.ds(8 * i, 8)]
 
-    def send_d(i, a, slot, src, dst):
+    def send_d(i, a, src, dst, to_mate):
         ref = piece(src, a, i)
-        return remote(ref, ref, sD.at[i, a, slot], rD.at[i, a, src], at_t(dst))
-
-    def wait_d(i, a, src):
-        ref = piece(src, a, i)
-        remote(ref, ref, sD.at[i, a, 0], rD.at[i, a, src], at_t(mate)).wait_recv()
+        remote(ref, ref, sD, rD.at[i, a, to_mate], at_t(dst)).start()
 
     def octet(c, p, a):
         return recvC[c, p, a].astype(F32)
@@ -185,18 +177,16 @@
     def start_d(i):
         for a in range(2):
             for k in (2, 1, 3):
-                send_d(i, a, k, t, lax.rem(t + 2 * k, 8)).start()
-            send_d(i, a, 0, t, mate).start()
+                send_d(i, a, t, lax.rem(t + 2 * k, 8), 0)
+            send_d(i, a, t, mate, 1)
 
     def relay_d(i, a):
+        got(XG.at[0:3, a, pl.ds(8 * i, 8)], rD.at[i, a, 0])
         for k in (1, 3, 2):
-            q = lax.rem(t + 2 * k, 8)
-            wait_d(i, a, q)
-            send_d(i, a, 4 + k, q, mate).start()
+            send_d(i, a, lax.rem(t + 2 * k, 8), mate, 1)
 
     def arrive_d(i, a):
-        for k in range(4):
-            wait_d(i, a, lax.rem(mate + 2 * k, 8))
+        got(XG.at[0:4, a, pl.ds(8 * i, 8)], rD.at[i, a, 1])
 
     for c in weights:
         c.wait()
@@ -212,7 +202,7 @@
         loop(rows // 128, one)
 
     flip(wd, wdT)
-    loop(32, wait_l)
+    got(recvR, rL)
 
     def rest(j):
         four = [recvR[4 * j + q].astype(F32) for q in range(4)]
@@ -223,17 +213,16 @@
     start_d(0)
 
     def prep(i):
-        c, first = lax.div(i - 1, 2), 16 * lax.rem(i + 1, 2)
-
-        def one(j):
-            p = first + 2 * j
-            wait_c(c, p)
-            wait_c(c, p + 1)
+        c, half = lax.div(i - 1, 2), lax.rem(i + 1, 2)
+        got(recvC.at[c, pl.ds(16 * half, 16)], rC.at[c, half])
+
+        def build(j):
+            p = 16 * half + 2 * j
             for a in range(2):
                 both = jnp.concatenate([octet(c, p, a), octet(c, p + 1, a)], axis=0)
                 XG[t, a, 8 * i + j] = both.astype(BF)
 
-        loop(8, one)
+        loop(8, build)
         start_d(i)
 
     def tile(i, owner, half):
@@ -254,15 +243,8 @@
             4: (part.at[u, tile(i, left, 0)], raw.at[1, i, u], left),
             5: (redS.at[1, i], red.at[1, i], left),
         }[m]
-        return remote(src, dst, sR.at[i, m, w % 2], rR.at[i, m, w % 2], peer(dev))
-
-    def rs_wait(i, m):
-        for w in (2,) if m % 3 == 2 else (0, 1):
-            dst = (rs1, raw, red)[m % 3].at[m // 3, i, UNITS[w]]
-            remote(dst, dst, sR.at[i, m, w % 2], rR.at[i, m, w % 2], peer(right)).wait_recv()
-
-    def rs_sends(i):
-        return [rs_send(i, m, w) for m in (0, 1, 3, 4) for w in (0, 1)] + [rs_send(i, 2), rs_send(i, 5)]
+        sem = rR.at[i, {0: 0, 3: 1}.get(m, 2)]
+        remote(src, dst, (sR1, sRaw, sRed)[m % 3], sem, peer(dev)).start()
 
     def rows_of(a, i):
         tiles = pl.ds(8 * i, 8)
@@ -276,12 +258,12 @@
         part[0, tiles] = nn(xs, wg[...]).astype(BF).reshape(8, 16, -1)
         part[1, tiles] = nn(xs, wu[...]).astype(BF).reshape(8, 16, -1)
         for m in (0, 3, 1, 4):
-            rs_send(i, m, 0).start()
+            rs_send(i, m, 0)
         relay_d(i, 1)
         arrive_d(i, 1)
         part[2, tiles] = nn(rows_of(1, i), wdT[...]).astype(BF).reshape(8, 16, -1)
         for m in (0, 3, 1, 4):
-            rs_send(i, m, 1).start()
+            rs_send(i, m, 1)
 
     def open_stage(i):
         @pl.when(i < S - 1)
@@ -295,12 +277,12 @@
     flip(wu, wuT)
 
     def middle(i):
-        rs_wait(i, 0)
+        got(rs1.at[0, i], rR.at[i, 0])
         redS[0, i] = (part[:, tile(i, right, 0)].astype(F32) + rs1[0, i].astype(F32)).astype(BF)
-        rs_send(i, 2).start()
-        rs_wait(i, 3)
+        rs_send(i, 2)
+        got(rs1.at[1, i], rR.at[i, 1])
         redS[1, i] = (part[:, tile(i, left, 1)].astype(F32) + rs1[1, i].astype(F32)).astype(BF)
-        rs_send(i, 5).start()
+        rs_send(i, 5)
 
     loop(S, middle)
 
@@ -312,34 +294,22 @@
     def hid_ref(n, owner, half=None):
         return H.at[0, HID[n], pl.ds(2 * owner, 2) if half is None else 2 * owner + half]
 
-    def ring(ref, i, m, sems):
+    def ring(ref, i, m, send, recv):
         src, dev = {
             0: (ref(i, d), right), 1: (ref(i, d), left),
             2: (ref(i, left, 0), right), 3: (ref(i, right, 1), left),
         }[m]
-        return remote(src, src, sems[0].at[i, m], sems[1].at[i, m], peer(dev))
-
-    def ring_wait(ref, i, m, sems):
-        dst = (ref(i, left), ref(i, right), ref(i, opp, 0), ref(i, opp, 1))[m]
-        remote(dst, dst, sems[0].at[i, m], sems[1].at[i, m], peer(right)).wait_recv()
+        remote(src, src, send, recv.at[i, min(m, 2)], peer(dev)).start()
 
     def ag_send(i, m):
-        return ring(ag_ref, i, m, (sG, rG))
-
-    def ag_wait(i, m):
-        ring_wait(ag_ref, i, m, (sG, rG))
+        ring(ag_ref, i, m, sG, rG)
 
     def hid_send(n, m):
-        return ring(hid_ref, n, m, (sN, rN))
-
-    def hid_wait(n, m):
-        ring_wait(hid_ref, n, m, (sN, rN))
+        ring(hid_ref, n, m, sN, rN)
 
     def own(i):
-        rs_wait(i, 1)
-        rs_wait(i, 4)
-        for half, (ra, rb, m) in enumerate(((red, raw, 2), (raw, red, 5))):
-            rs_wait(i, m)
+        got(raw.at[:, 0:2], rR.at[i, 2])
+        for half, (ra, rb) in enumerate(((red, raw), (raw, red))):
             at, to = tile(i, d, half), 2 * d + half
             gate, up, grad = (
                 part[u, at].astype(F32) + ra[0, i, u].astype(F32) + rb[1, i, u].astype(F32)
@@ -350,73 +320,66 @@
             H[0, i, to] = (silu * up).astype(BF)
             H[1, i, to] = (grad * up * s * (1.0 + gate * (1.0 - s))).astype(BF)
             H[2, i, to] = (grad * silu).astype(BF)
-        ag_send(i, 0).start()
-        ag_send(i, 1).start()
+        ag_send(i, 0)
+        ag_send(i, 1)
 
     def relay(i):
-        ag_wait(i, 0)
-        ag_send(i, 2).start()
-        ag_wait(i, 1)
-        ag_send(i, 3).start()
-
-    def p_copy(i):
-        return remote(rgp.at[i, 1 - core], recvP.at[i], sP.at[i], rP.at[i], at_t(mate))
+        for m, owner in enumerate((left, right)):
+            got(ag_ref(i, owner), rG.at[i, m])
+            ag_send(i, m + 2)
 
     def q_send(i, k):
         yy = lax.rem(y + k, 4)
-        return remote(qs.at[i, yy], recvQ.at[i, y], sQ.at[i, yy], rQ.at[i, y], at_t(2 * yy + core))
+        remote(qs.at[i, yy], recvQ.at[i, y], sQ, rQ.at[i], at_t(2 * yy + core)).start()
 
     def hid(u, i):
         return H[u, i].reshape(128, -1)
 
     def rows(i):
-        ag_wait(i, 2)
-        ag_wait(i, 3)
+        got(H.at[1:3, i, 0:2], rG.at[i, 2])
         rg = nn(hid(1, i), wgT[...]) + nn(hid(2, i), wuT[...])
         for q in range(8):
             rgp[i, q % 2, q // 2] = rg[:, 128 * q : 128 * q + 128].astype(BF)
-        p_copy(i).start()
+        remote(rgp.at[i, 1 - core], recvP.at[i], sP, rP.at[i], at_t(mate)).start()
 
     def pair(i):
-        remote(recvP.at[i], recvP.at[i], sP.at[i], rP.at[i], at_t(mate)).wait_recv()
+        got(recvP.at[i], rP.at[i])
         qs[i] = (rgp[i, core].astype(F32) + recvP[i].astype(F32)).astype(BF)
         for k in (2, 1, 3):
-            q_send(i, k).start()
-
-    def z_main(i, o):
-        c, p = lax.div(i + 1, 2), 16 * lax.rem(i + 1, 2) + o
-        return c, p, remote(zs.at[i, o], recvZ.at[c, b], sZ.at[c, p], rZ.at[c, b], at_p(p))
-
-    def z_rest(p):
-        return remote(zs.at[0, lax.div(p, 2)], recvZ.at[0, b], sZ.at[0, p], rZ.at[0, b], at_p(p))
+            q_send(i, k)
 
     def back(i):
         tot = qs[i, y].astype(F32)
-        for k in (1, 3, 2):
-            yy = lax.rem(y + k, 4)
-            remote(recvQ.at[i, yy], recvQ.at[i, yy], sQ.at[i, yy], rQ.at[i, yy], at_t(mate)).wait_recv()
-            tot = tot + recvQ[i, yy].astype(F32)
+        got(recvQ.at[i, 0:3], rQ.at[i])
+        for k in range(1, 4):
+            tot = tot + recvQ[i, lax.rem(y + k, 4)].astype(F32)
         zs[i] = tot.reshape(16, 8, 128).astype(BF)
 
         @pl.when(i > 0)
         def _():
-            def one(o):
-                c, p, copy = z_main(i, o)
+            c = lax.div(i + 1, 2)
+
+            def put(o):
+                p = 16 * lax.rem(i + 1, 2) + o
 
                 @pl.when(p != b)
                 def _():
-                    copy.start()
+                    remote(zs.at[i, o], recvZ.at[c, b], sZ, rZ, at_p(p)).start()
 
                 @pl.when(p == b)
                 def _():
-                    recvZ[c, b] = zs[i, o]
-
-            loop(16, one)
+                    pltpu.make_async_copy(zs.at[i, o], recvZ.at[c, b], rZ).start()
+
+            loop(16, put)
 
         @pl.when(i == 0)
         def _():
-            loop(31, lambda k: z_rest(far_first(k)).start())
-            recvZ[0, b] = zs[0, lax.div(b, 2)]
+            def put(k):
+                p = far_first(k)
+                remote(zs.at[0, lax.div(p, 2)], recvZ.at[0, b], sZ, rZ, at_p(p)).start()
+
+            loop(31, put)
+            pltpu.make_async_copy(zs.at[0, lax.div(b, 2)], recvZ.at[0, b], rZ).start()
 
     def turn(i):
         for q in range(8):
@@ -437,20 +400,22 @@
     own(1)
     own(2)
     relay(0)
+    relay(1)
 
     def cycle(i):
         @pl.when(i + 3 < S)
         def _():
             own(i + 3)
 
-        @pl.when(i + 1 < S)
-        def _():
-            relay(i + 1)
-
-        @pl.when(i == S - 2)
-        def _():
-            for m in (0, 1):
-                hid_send(0, m).start()
+        @pl.when(i + 2 < S)
+        def _():
+            relay(i + 2)
+
+        @pl.when(i == S - 3)
+        def _():
+            for n in (0, 1):
+                for m in (0, 1):
+                    hid_send(n, m)
 
         @pl.when(i >= 1)
         def _():
@@ -467,90 +432,50 @@
     back(S - 2)
     model_grad(1, gg_out)
     back(S - 1)
-    for n in (1, 2):
-        for m in (0, 1):
-            hid_send(n, m).start()
+    for m in (0, 1):
+        hid_send(2, m)
 
     def hid_relay(n):
-        for m in (0, 1):
-            hid_wait(n, m)
-            hid_send(n, m + 2).start()
+        for m, owner in enumerate((left, right)):
+            got(hid_ref(n, owner), rN.at[n, m])
+            hid_send(n, m + 2)
 
     hid_relay(0)
+    hid_relay(1)
     model_grad(2, gu_out)
-    hid_relay(1)
     hid_relay(2)
 
-    def wait_z(k):
-        p = lax.rem(b + k, 32)
-        for c in range(3):
-            ref = recvZ.at[c, p]
-            remote(ref, ref, sZ.at[c, p], rZ.at[c, p], at_p(p)).wait_recv()
-
-    loop(32, wait_z, 1)
+    got(recvZ, rZ)
     for dd in range(4):
         z = recvZ[:, 8 * dd : 8 * dd + 8].astype(F32).reshape(PLACES, 128).astype(BF)
         part_rows = nn(tab[...], z).reshape(8, 8, 128).astype(BF)
         sendY[:, :, 128 * dd : 128 * dd + 128] = part_rows
 
-    def y_copy(k):
+    def y_send(k):
         q = lax.rem(t + k, 8)
-        return remote(sendY.at[q], recvY.at[t], sY.at[q], rY.at[t], at_t(q))
-
-    loop(8, lambda k: y_copy(k).start(), 1)
+        remote(sendY.at[q], recvY.at[t], sY, rY, at_t(q)).start()
+
+    loop(8, y_send, 1)
     recvY[t] = sendY[t]
     for n in (0, 1):
-        for m in (2, 3):
-            hid_wait(n, m)
+        got(H.at[0, HID[n], 0:2], rN.at[n, 2])
     accd[...] = down_part(0, 4)
 
-    loop(8, lambda k: send_a(k).wait_send(), 1)
-    loop(31, lambda k: send_l(k).wait_send())
-    for c in range(2):
-        loop(31, lambda k, c=c: send_c(c, k).wait_send())
-
-    def drain(i):
-        for a in range(2):
-            for k in (0, 1, 2, 3, 5, 6, 7):
-                send_d(i, a, k, t, mate).wait_send()
-        for k in range(1, 4):
-            q_send(i, k).wait_send()
-        for c in rs_sends(i):
-            c.wait_send()
-        for m in range(4):
-            ag_send(i, m).wait_send()
-        p_copy(i).wait_send()
-
-        @pl.when(i > 0)
-        def _():
-            def one(o):
-                c, p, copy = z_main(i, o)
-
-                @pl.when(p != b)
-                def _():
-                    copy.wait_send()
-
-            loop(16, one)
-
-    loop(S, drain)
-    loop(31, lambda k: z_rest(far_first(k)).wait_send())
-
-    def wait_y(k):
-        q = lax.rem(t + k, 8)
-        remote(recvY.at[q], recvY.at[q], sY.at[q], rY.at[q], at_t(q)).wait_recv()
-
-    loop(8, wait_y, 1)
+    for ref, sem in (
+        (recvA.at[0:7], sA), (recvR.at[0:31], sL), (recvC.at[:, 0:31], sC), (XG.at[0:7], sD),
+        (rs1, sR1), (raw, sRaw), (red, sRed), (H.at[1:3, :, 0:6], sG), (recvP, sP),
+        (recvQ.at[:, 0:3], sQ), (recvZ.at[:, 0:31], sZ),
+    ):
+        sent(ref, sem)
+    got(recvY.at[0:7], rY)
     for dd in range(4):
         for q in range(8):
             at = slice(1024 * dd + 128 * q, 1024 * dd + 128 * q + 128)
             y_out[:, at] = recvY[q, :, 128 * dd : 128 * dd + 128]
-    loop(8, lambda k: y_copy(k).wait_send(), 1)
-    for m in (2, 3):
-        hid_wait(2, m)
+    got(H.at[0, HID[2], 0:2], rN.at[2, 2])
     gd_out[0] = (accd[...] + down_part(4, S)).astype(BF)
-    for n in range(3):
-        for m in range(4):
-            hid_send(n, m).wait_send()
+    sent(recvY.at[0:7], sY)
+    sent(H.at[0, :, 0:6], sN)
 
 
 def put_out(*refs):
@@ -595,10 +520,8 @@
             buf(S, 2, 4, 128, 128), buf(S, 4, 128, 128), buf(S, 4, 128, 128), buf(S, 4, 128, 128),
             buf(S, 16, 8, 128), buf(3, 32, 8, 128), buf(8, 8, 512), buf(8, 8, 512),
             buf(fl, dl, dtype=F32),
-            dma((5,)), dma((3,)), dma((8,)), dma((8,)), dma((32,)), dma((32,)), dma((2, 32)), dma((2, 32)),
-            dma((S, 2, 8)), dma((S, 2, 8)), dma((S, 6, 2)), dma((S, 6, 2)), dma((S, 4)), dma((S, 4)),
-            dma((3, 4)), dma((3, 4)), dma((S,)), dma((S,)), dma((S, 4)), dma((S, 4)), dma((3, 32)), dma((3, 32)),
-            dma((8,)), dma((8,)),
+            dma((5,)), dma((3,)), dma((17,)), dma((2, 2)), dma((S, 2, 2)),
+            dma((S, 3)), dma((S, 3)), dma((3, 3)), dma((S,)), dma((S,)),
         ],
         compiler_params=pltpu.CompilerParams(
             collective_id=0, has_side_effects=True, vmem_limit_bytes=48 * 1024 * 1024

time: 164 us -> 153 us (0.933)
  Pallas kernels: 162 us -> 153 us
    pallas_call x1, Pallas kernels: 160 us -> 150 us  [shards(): pl.pallas_call(kernel, name='expert_back', out_shape=(jax.ShapeDtypeStruc...]
where the time goes in v5:
time: 153 us
  Pallas kernels  153 us (100%)
    pallas_call x1, Pallas kernels, shards(): pl.pallas_call(kernel, name='expert_back', out_shape=(jax.ShapeDtypeStruc...  150 us

profile of v5, /device:TPU:1, one launch (start us, length us, event | category | flops | bytes accessed | tf_op | source)
XLA Modules:
  0.0 153.4 jit_solution(14577897943444144951)
XLA Ops:
  0.6 150.2 %expert_back.1 = (bf16[8,4096]{1,0:T(8,128)(2,1)S(1)}, bf16[1,1024,896]{2,1,0:T(8,128)(2,1)S(1)}, bf16[1,1024,896]{2,1,0:T(8,128)(2,1)S(1)}, bf16[1,896,1024]{2,1,0:T(8,128)(2,1)S(1)}) custom-call(bf16[8,4096]{1,0:T(8,128)(2,1)} %tok_hbm.1, bf16[8,4096]{1,0:T(8,128)(2,1)} %og_hbm.1, f32[2,64]{1,0:T(2,128)} %bitcast.9, s32[2,64]{1,0:T(2,128)} %bitcast.10, ...), custom_call_target="tpu_custom_call" | custom-call | tf_op jit(solution)/shard_map/expert_back/pallas_call | solution.py:500
  150.9 2.5 %put_out.1 = (bf16[8,4096]{1,0:T(8,128)(2,1)}, bf16[1,1024,896]{2,1,0:T(8,128)(2,1)}, bf16[1,1024,896]{2,1,0:T(8,128)(2,1)}, bf16[1,896,1024]{2,1,0:T(8,128)(2,1)}) custom-call(bf16[8,4096]{1,0:T(8,128)(2,1)S(1)} %get-tuple-element.8.refs_0_, bf16[1,1024,896]{2,1,0:T(8,128)(2,1)S(1)} %get-tuple-element.9.refs_1_, ...), custom_call_target="tpu_custom_call" | custom-call | tf_op jit(solution)/shard_map/put_out/pallas_call | solution.py:533

commit v6 on v5

--- a/solution.py
+++ b/solution.py
@@ -47,11 +47,11 @@
 
 def kernel(
     tok_hbm, og_hbm, prob_hbm, id_hbm, slot_hbm, wg_hbm, wu_hbm, wd_hbm,
-    y_out, gg_out, gu_out, gd_out,
+    y_out, gg_out, gu_out, accd, h_last, g_last,
     tok, og, prob, ids, slots, wg, wu, wd, wgT, wuT, wdT, tab,
-    sendA, recvA, sendR, recvR, sendC, recvC, XG, XT, part, rs1, raw, red, redS, H,
-    rgp, recvP, qs, recvQ, zs, recvZ, sendY, recvY, accd,
-    isem, wsem, one, rC, rD, rR, rG, rN, rP, rQ,
+    sendA, recvA, sendR, recvR, sendC, XG, XT, part, rs1, raw, red, redS, H,
+    rgp, recvP, qs, recvQ, zs, zr, recvZ, recvZr, sendY, recvY,
+    isem, wsem, one, rA, rC, rD, rR, rG, rN, rP, rQ,
 ):
     d, e, t = lax.axis_index("dp"), lax.axis_index("expert"), lax.axis_index("tensor")
     b = d * 8 + e
@@ -59,8 +59,8 @@
     mate = t + 1 - 2 * core
     right, left, opp = lax.rem(d + 1, 4), lax.rem(d + 3, 4), lax.rem(d + 2, 4)
 
-    sA, rA, sL, rL, sC, sD, sR1, sRaw, sRed, sG, sN, sP, sQ, sZ, rZ, sY, rY = (
-        one.at[n] for n in range(17)
+    sA, sL, rL, sC, sD, sR1, sRaw, sRed, sG, sN, sP, sQ, sZ, rZ, sZr, rZr, sY, rY = (
+        one.at[n] for n in range(18)
     )
 
     def at_t(tt):
@@ -111,11 +111,11 @@
     for dd in range(4):
         for q in range(8):
             at = slice(1024 * dd + 128 * q, 1024 * dd + 128 * q + 128)
-            sendA[q, 0, :, 128 * dd : 128 * dd + 128] = tok[:, at]
-            sendA[q, 1, :, 128 * dd : 128 * dd + 128] = og[:, at]
+            sendA[0, q, :, 128 * dd : 128 * dd + 128] = tok[:, at]
+            sendA[1, q, :, 128 * dd : 128 * dd + 128] = og[:, at]
     slot, owner = slots[...], ids[...] * 8
     past = slot >= 16
-    low = jnp.where(slot < 8, 64 + owner + slot, 120 + owner + slot)
+    low = 64 + 2 * owner + slot
 
     def places(extra):
         return jnp.where(slot < CAP, jnp.where(past, owner + slot - 16 + extra, low), -1)
@@ -127,26 +127,68 @@
     by_token = lax.broadcasted_iota(jnp.int32, (64, PLACES), 1)
     tab[...] = sum((by_token == column(place_z[k : k + 1])).astype(F32) for k in range(2)).astype(BF)
     p0, p1 = (column(prob[k : k + 1]) for k in range(2))
+    for c in weights:
+        c.wait()
+
+    def flip(src, dst):
+        rows, cols = src.shape
+
+        def one(r):
+            at = pl.ds(pl.multiple_of(128 * r, 128), 128)
+            for f in range(cols // 128):
+                dst[128 * f : 128 * f + 128, at] = src[at, 128 * f : 128 * f + 128].T
+
+        loop(rows // 128, one)
+
+    flip(wd, wdT)
     pl.semaphore_wait(bar, 38)
 
-    def send_a(k):
-        q = lax.rem(t + k, 8)
-        remote(sendA.at[q], recvA.at[t], sA, rA, at_t(q)).start()
-
-    loop(8, send_a, 1)
-    recvA[t] = sendA[t]
-    got(recvA.at[0:7], rA)
-
-    rx = recvA[:, 0].astype(F32).reshape(64, 512).astype(BF)
-    ry = recvA[:, 1].astype(F32).reshape(64, 512)
-    xb = nn(tx, rx)
-    gb = nn(t0, (p0 * ry).astype(BF)) + nn(t1, (p1 * ry).astype(BF))
+    for a in range(2):
+        def send_a(k, a=a):
+            q = lax.rem(t + k, 8)
+            remote(sendA.at[a, q], recvA.at[a, t], sA, rA.at[a], at_t(q)).start()
+
+        loop(8, send_a, 1)
+        recvA[a, t] = sendA[a, t]
+
+    got(recvA.at[0, 0:7], rA.at[0])
+    rx = recvA[0].astype(F32).reshape(64, 512).astype(BF)
+
+    z0, x0 = 2 * d + lax.div(e, 4), lax.rem(e, 4)
+    FAR = (4, 3, 5, 2, 6, 1, 7, 0)
+
+    def device_at(dz, dx):
+        z = lax.rem(z0 + dz, 8)
+        return lax.div(z, 2), 4 * lax.rem(z, 2) + lax.rem(x0 + dx, 4)
+
+    def send_stage(delta, a):
+        i, dx = delta + delta // 2, (4 - delta) % 4
+        for dz in FAR:
+            pd, pe = device_at(dz, dx)
+            src, dst = sendC.at[a, 8 * pd + pe], XG.at[t, a, 8 * i + z0]
+            if dz or dx:
+                remote(src, dst, sC, rC.at[i, a], (pd, pe, t)).start()
+            else:
+                pltpu.make_async_copy(src, dst, rC.at[i, a]).start()
+
+    def put_slots(a, v):
+        for dd in range(4):
+            cols = slice(128 * dd, 128 * dd + 128)
+            sendC[a, 8 * dd : 8 * dd + 8] = v[:, cols].reshape(8, 16, 128).astype(BF)
+
+    put_slots(0, nn(tx[64:], rx))
+    send_stage(0, 0)
+    got(recvA.at[1, 0:7], rA.at[1])
+    ry = recvA[1].astype(F32).reshape(64, 512)
+    s0, s1 = (p0 * ry).astype(BF), (p1 * ry).astype(BF)
+    put_slots(1, nn(t0[64:], s0) + nn(t1[64:], s1))
+    send_stage(0, 1)
+    for a in range(2):
+        send_stage(1, a)
+    xb, gb = nn(tx[:64], rx), nn(t0[:64], s0) + nn(t1[:64], s1)
     for dd in range(4):
-        cols, to = slice(128 * dd, 128 * dd + 128), slice(8 * dd, 8 * dd + 8)
-        sendR[to] = (xb[:64, cols] + gb[:64, cols]).reshape(8, 8, 128).astype(BF)
-        for c in range(2):
-            for a, v in enumerate((xb, gb)):
-                sendC[c, to, a] = v[64 * c + 64 : 64 * c + 128, cols].reshape(8, 8, 128).astype(BF)
+        cols = slice(128 * dd, 128 * dd + 128)
+        sendR[8 * dd : 8 * dd + 8] = (xb[:, cols] + gb[:, cols]).reshape(8, 8, 128).astype(BF)
 
     def send_l(k):
         p = far_first(k)
@@ -154,15 +196,9 @@
 
     loop(31, send_l)
     pltpu.make_async_copy(sendR.at[b], recvR.at[b], rL).start()
-    for c in range(2):
-        sem = rC.at[c, lax.div(d, 2)]
-
-        def send_c(k, c=c, sem=sem):
-            p = far_first(k)
-            remote(sendC.at[c, p], recvC.at[c, b], sC, sem, at_p(p)).start()
-
-        loop(31, send_c)
-        pltpu.make_async_copy(sendC.at[c, b], recvC.at[c, b], sem).start()
+    for delta in (2, 3):
+        for a in range(2):
+            send_stage(delta, a)
 
     def piece(src, a, i):
         return XG.at[src, a, pl.ds(8 * i, 8)]
@@ -171,14 +207,10 @@
         ref = piece(src, a, i)
         remote(ref, ref, sD, rD.at[i, a, to_mate], at_t(dst)).start()
 
-    def octet(c, p, a):
-        return recvC[c, p, a].astype(F32)
-
-    def start_d(i):
-        for a in range(2):
-            for k in (2, 1, 3):
-                send_d(i, a, t, lax.rem(t + 2 * k, 8), 0)
-            send_d(i, a, t, mate, 1)
+    def start_d(i, a):
+        for k in (2, 1, 3):
+            send_d(i, a, t, lax.rem(t + 2 * k, 8), 0)
+        send_d(i, a, t, mate, 1)
 
     def relay_d(i, a):
         got(XG.at[0:3, a, pl.ds(8 * i, 8)], rD.at[i, a, 0])
@@ -188,42 +220,25 @@
     def arrive_d(i, a):
         got(XG.at[0:4, a, pl.ds(8 * i, 8)], rD.at[i, a, 1])
 
-    for c in weights:
-        c.wait()
-
-    def flip(src, dst):
-        rows, cols = src.shape
-
-        def one(r):
-            at = pl.ds(pl.multiple_of(128 * r, 128), 128)
-            for f in range(cols // 128):
-                dst[128 * f : 128 * f + 128, at] = src[at, 128 * f : 128 * f + 128].T
-
-        loop(rows // 128, one)
-
-    flip(wd, wdT)
-    got(recvR, rL)
-
     def rest(j):
         four = [recvR[4 * j + q].astype(F32) for q in range(4)]
         for a in range(2):
-            XG[t, a, j] = jnp.concatenate([v[4 * a : 4 * a + 4] for v in four], axis=0).astype(BF)
-
-    loop(8, rest)
-    start_d(0)
+            XG[t, a, 16 + j] = jnp.concatenate([v[4 * a : 4 * a + 4] for v in four], axis=0).astype(BF)
 
     def prep(i):
-        c, half = lax.div(i - 1, 2), lax.rem(i + 1, 2)
-        got(recvC.at[c, pl.ds(16 * half, 16)], rC.at[c, half])
-
-        def build(j):
-            p = 16 * half + 2 * j
-            for a in range(2):
-                both = jnp.concatenate([octet(c, p, a), octet(c, p + 1, a)], axis=0)
-                XG[t, a, 8 * i + j] = both.astype(BF)
-
-        loop(8, build)
-        start_d(i)
+        @pl.when(i == 2)
+        def _():
+            got(recvR, rL)
+            loop(8, rest)
+
+        for a in range(2):
+            @pl.when(i != 2)
+            def _(a=a):
+                got(XG.at[t, a, pl.ds(8 * i, 8)], rC.at[i, a])
+
+            start_d(i, a)
+
+    prep(0)
 
     def tile(i, owner, half):
         return 8 * i + 2 * owner + half
@@ -231,9 +246,9 @@
     def peer(dd):
         return (dd, e, t)
 
-    UNITS = (slice(0, 2), slice(2, 3), slice(0, 3))
-
-    def rs_send(i, m, w=2):
+    UNITS = (slice(0, 1), slice(1, 2), slice(2, 3), slice(0, 3))
+
+    def rs_send(i, m, w=3):
         u = UNITS[w]
         src, dst, dev = {
             0: (part.at[u, tile(i, opp, 0)], rs1.at[0, i, u], right),
@@ -255,15 +270,15 @@
         relay_d(i, 0)
         arrive_d(i, 0)
         xs = rows_of(0, i)
-        part[0, tiles] = nn(xs, wg[...]).astype(BF).reshape(8, 16, -1)
-        part[1, tiles] = nn(xs, wu[...]).astype(BF).reshape(8, 16, -1)
-        for m in (0, 3, 1, 4):
-            rs_send(i, m, 0)
+        for w, wt in enumerate((wg, wu)):
+            part[w, tiles] = nn(xs, wt[...]).astype(BF).reshape(8, 16, -1)
+            for m in (0, 3, 1, 4):
+                rs_send(i, m, w)
         relay_d(i, 1)
         arrive_d(i, 1)
         part[2, tiles] = nn(rows_of(1, i), wdT[...]).astype(BF).reshape(8, 16, -1)
         for m in (0, 3, 1, 4):
-            rs_send(i, m, 1)
+            rs_send(i, m, 2)
 
     def open_stage(i):
         @pl.when(i < S - 1)
@@ -353,33 +368,34 @@
         got(recvQ.at[i, 0:3], rQ.at[i])
         for k in range(1, 4):
             tot = tot + recvQ[i, lax.rem(y + k, 4)].astype(F32)
-        zs[i] = tot.reshape(16, 8, 128).astype(BF)
-
-        @pl.when(i > 0)
-        def _():
-            c = lax.div(i + 1, 2)
-
-            def put(o):
-                p = 16 * lax.rem(i + 1, 2) + o
-
-                @pl.when(p != b)
-                def _():
-                    remote(zs.at[i, o], recvZ.at[c, b], sZ, rZ, at_p(p)).start()
-
-                @pl.when(p == b)
-                def _():
-                    pltpu.make_async_copy(zs.at[i, o], recvZ.at[c, b], rZ).start()
-
-            loop(16, put)
-
-        @pl.when(i == 0)
-        def _():
+        @pl.when(i != 2)
+        def _():
+            zs[i] = tot.reshape(8, 16, 128).astype(BF)
+            x = lax.rem(x0 + i - lax.div(i, 3), 4)
+            for dz in FAR:
+                z = lax.rem(z0 + dz, 8)
+                pd, pe = lax.div(z, 2), 4 * lax.rem(z, 2) + x
+                if dz:
+                    remote(zs.at[i, z], recvZ.at[b], sZ, rZ, (pd, pe, t)).start()
+                else:
+                    @pl.when(i != 0)
+                    def _():
+                        remote(zs.at[i, z], recvZ.at[b], sZ, rZ, (pd, pe, t)).start()
+
+                    @pl.when(i == 0)
+                    def _():
+                        pltpu.make_async_copy(zs.at[i, z], recvZ.at[b], rZ).start()
+
+        @pl.when(i == 2)
+        def _():
+            zr[...] = tot.reshape(16, 8, 128).astype(BF)
+
             def put(k):
                 p = far_first(k)
-                remote(zs.at[0, lax.div(p, 2)], recvZ.at[0, b], sZ, rZ, at_p(p)).start()
+                remote(zr.at[lax.div(p, 2)], recvZr.at[b], sZr, rZr, at_p(p)).start()
 
             loop(31, put)
-            pltpu.make_async_copy(zs.at[0, lax.div(b, 2)], recvZ.at[0, b], rZ).start()
+            pltpu.make_async_copy(zr.at[lax.div(b, 2)], recvZr.at[b], rZr).start()
 
     def turn(i):
         for q in range(8):
@@ -428,26 +444,27 @@
         rows(i)
 
     loop(S, cycle)
+    def hid_relay(n):
+        for m, owner in enumerate((left, right)):
+            got(hid_ref(n, owner), rN.at[n, m])
+            hid_send(n, m + 2)
+
     pair(S - 1)
     back(S - 2)
     model_grad(1, gg_out)
     back(S - 1)
     for m in (0, 1):
         hid_send(2, m)
-
-    def hid_relay(n):
-        for m, owner in enumerate((left, right)):
-            got(hid_ref(n, owner), rN.at[n, m])
-            hid_send(n, m + 2)
-
     hid_relay(0)
     hid_relay(1)
-    model_grad(2, gu_out)
     hid_relay(2)
 
     got(recvZ, rZ)
+    got(recvZr, rZr)
     for dd in range(4):
-        z = recvZ[:, 8 * dd : 8 * dd + 8].astype(F32).reshape(PLACES, 128).astype(BF)
+        at = slice(8 * dd, 8 * dd + 8)
+        past16 = recvZr[at].astype(F32).reshape(64, 128).astype(BF)
+        z = jnp.concatenate([past16, recvZ[at].reshape(128, 128)], axis=0)
         part_rows = nn(tab[...], z).reshape(8, 8, 128).astype(BF)
         sendY[:, :, 128 * dd : 128 * dd + 128] = part_rows
 
@@ -457,14 +474,16 @@
 
     loop(8, y_send, 1)
     recvY[t] = sendY[t]
+    model_grad(2, gu_out)
     for n in (0, 1):
         got(H.at[0, HID[n], 0:2], rN.at[n, 2])
     accd[...] = down_part(0, 4)
+    g_last[...] = rows_of(1, 4)
 
     for ref, sem in (
-        (recvA.at[0:7], sA), (recvR.at[0:31], sL), (recvC.at[:, 0:31], sC), (XG.at[0:7], sD),
+        (recvA.at[:, 0:7], sA), (recvR.at[0:31], sL), (sendC.at[:, 0:31], sC), (XG.at[0:7], sD),
         (rs1, sR1), (raw, sRaw), (red, sRed), (H.at[1:3, :, 0:6], sG), (recvP, sP),
-        (recvQ.at[:, 0:3], sQ), (recvZ.at[:, 0:31], sZ),
+        (recvQ.at[:, 0:3], sQ), (recvZ.at[0:31], sZ), (recvZr.at[0:31], sZr),
     ):
         sent(ref, sem)
     got(recvY.at[0:7], rY)
@@ -473,16 +492,20 @@
             at = slice(1024 * dd + 128 * q, 1024 * dd + 128 * q + 128)
             y_out[:, at] = recvY[q, :, 128 * dd : 128 * dd + 128]
     got(H.at[0, HID[2], 0:2], rN.at[2, 2])
-    gd_out[0] = (accd[...] + down_part(4, S)).astype(BF)
+    h_last[...] = H[0, 4].reshape(128, -1)
     sent(recvY.at[0:7], sY)
     sent(H.at[0, :, 0:6], sN)
 
 
-def put_out(*refs):
-    sems = refs[8]
-    copies = [pltpu.make_async_copy(refs[n], refs[4 + n], sems.at[n]) for n in range(4)]
-    for c in copies:
+def put_out(yv, gg, gu, accd, h_last, g_last, y_out, gg_out, gu_out, gd_out, gd, sems):
+    copies = [
+        pltpu.make_async_copy(src, dst, sems.at[n])
+        for n, (src, dst) in enumerate(((gg, gg_out), (gu, gu_out), (yv, y_out), (gd, gd_out)))
+    ]
+    for c in copies[:3]:
         c.start()
+    gd[0] = (accd[...] + tn(h_last[...], g_last[...])).astype(BF)
+    copies[3].start()
     for c in copies:
         c.wait()
 
@@ -497,34 +520,35 @@
     def buf(*shape, dtype=BF):
         return pltpu.VMEM(shape, dtype)
 
-    yv, gg, gu, gd = pl.pallas_call(
+    parts = pl.pallas_call(
         kernel,
         name="expert_back",
         out_shape=(
             jax.ShapeDtypeStruct(tokens.shape, BF),
             jax.ShapeDtypeStruct(w_gate.shape, BF),
             jax.ShapeDtypeStruct(w_up.shape, BF),
-            jax.ShapeDtypeStruct(w_down.shape, BF),
+            jax.ShapeDtypeStruct((fl, dl), F32),
+            jax.ShapeDtypeStruct((128, fl), BF),
+            jax.ShapeDtypeStruct((128, dl), BF),
         ),
         in_specs=[hbm] * 8,
-        out_specs=(vm, vm, vm, vm),
+        out_specs=(vm,) * 6,
         scratch_shapes=[
             buf(8, 4096), buf(8, 4096), buf(2, 64, dtype=F32),
             buf(2, 64, dtype=jnp.int32), buf(2, 64, dtype=jnp.int32),
             buf(dl, fl), buf(dl, fl), buf(fl, dl), buf(fl, dl), buf(fl, dl), buf(dl, fl), buf(64, PLACES),
-            buf(8, 2, 8, 512), buf(8, 2, 8, 512),
-            buf(32, 8, 128), buf(32, 8, 128), buf(2, 32, 2, 8, 128), buf(2, 32, 2, 8, 128),
+            buf(2, 8, 8, 512), buf(2, 8, 8, 512),
+            buf(32, 8, 128), buf(32, 8, 128), buf(2, 32, 16, 128),
             buf(8, 2, 40, 16, 128), buf(dl, 640), buf(3, 40, 16, fl),
             buf(2, S, 3, 16, fl), buf(2, S, 3, 16, fl), buf(2, S, 3, 16, fl), buf(2, S, 3, 16, fl),
             buf(3, S, 8, 16, fl),
             buf(S, 2, 4, 128, 128), buf(S, 4, 128, 128), buf(S, 4, 128, 128), buf(S, 4, 128, 128),
-            buf(S, 16, 8, 128), buf(3, 32, 8, 128), buf(8, 8, 512), buf(8, 8, 512),
-            buf(fl, dl, dtype=F32),
-            dma((5,)), dma((3,)), dma((17,)), dma((2, 2)), dma((S, 2, 2)),
+            buf(S, 8, 16, 128), buf(16, 8, 128), buf(32, 16, 128), buf(32, 8, 128), buf(8, 8, 512), buf(8, 8, 512),
+            dma((5,)), dma((3,)), dma((18,)), dma((2,)), dma((S, 2)), dma((S, 2, 2)),
             dma((S, 3)), dma((S, 3)), dma((3, 3)), dma((S,)), dma((S,)),
         ],
         compiler_params=pltpu.CompilerParams(
-            collective_id=0, has_side_effects=True, vmem_limit_bytes=48 * 1024 * 1024
+            collective_id=0, has_side_effects=True, vmem_limit_bytes=46 * 1024 * 1024
         ),
     )(*(
         pltpu.with_memory_space_constraint(v, pltpu.HBM)
@@ -533,12 +557,14 @@
     return pl.pallas_call(
         put_out,
         name="put_out",
-        out_shape=tuple(jax.ShapeDtypeStruct(v.shape, v.dtype) for v in (yv, gg, gu, gd)),
-        in_specs=[hbm] * 4,
+        out_shape=tuple(
+            jax.ShapeDtypeStruct(v.shape, BF) for v in (tokens, w_gate, w_up, w_down)
+        ),
+        in_specs=[vm] * 6,
         out_specs=(hbm,) * 4,
-        scratch_shapes=[dma((4,))],
-        compiler_params=pltpu.CompilerParams(vmem_limit_bytes=1024 * 1024),
-    )(yv, gg, gu, gd)
+        scratch_shapes=[buf(*w_down.shape), dma((4,))],
+        compiler_params=pltpu.CompilerParams(vmem_limit_bytes=16 * 1024 * 1024),
+    )(*parts)
 
 
 def solution(mesh):

time: 153 us -> 152 us (level)
  no operation moved by 1% of the time
where the time goes in v6:
time: 152 us
  Pallas kernels  152 us (100%)
    pallas_call x1, Pallas kernels, shards(): pl.pallas_call(kernel, name='expert_back', out_shape=(jax.ShapeDtypeStruc...  149 us

profile of v6, /device:TPU:1, one launch (start us, length us, event | category | flops | bytes accessed | tf_op | source)
XLA Modules:
  0.0 152.2 jit_solution(5532741682522023757)
XLA Ops:
  0.6 149.1 %expert_back.1 = (bf16[8,4096]{1,0:T(8,128)(2,1)S(1)}, bf16[1,1024,896]{2,1,0:T(8,128)(2,1)S(1)}, bf16[1,1024,896]{2,1,0:T(8,128)(2,1)S(1)}, f32[896,1024]{1,0:T...) custom-call(bf16[8,4096]{1,0:T(8,128)(2,1)} %tok_hbm.1, bf16[8,4096]{1,0:T(8,128)(2,1)} %og_hbm.1, ...), custom_call_target="tpu_custom_call" | custom-call | tf_op jit(solution)/shard_map/expert_back/pallas_call | solution.py:523
  149.7 2.5 %put_out.1 = (bf16[8,4096]{1,0:T(8,128)(2,1)}, bf16[1,1024,896]{2,1,0:T(8,128)(2,1)}, bf16[1,1024,896]{2,1,0:T(8,128)(2,1)}, bf16[1,896,1024]{2,1,0:T(8,128)(2,1)}) custom-call(bf16[8,4096]{1,0:T(8,128)(2,1)S(1)} %get-tuple-element.10.yv, bf16[1,1024,896]{2,1,0:T(8,128)(2,1)S(1)} %get-tuple-element.11.gg, bf16[1,1024,896]{2,1,0:T(8,128)(2,1)S(1)} %get-tuple-element.12.gu, ...), custom_call_target="tpu_custom_call" | custom-call | tf_op jit(solution)/shard_map/put_out/pallas_call | solution.py:557

commit v7 on v6

--- a/solution.py
+++ b/solution.py
@@ -148,7 +148,8 @@
             q = lax.rem(t + k, 8)
             remote(sendA.at[a, q], recvA.at[a, t], sA, rA.at[a], at_t(q)).start()
 
-        loop(8, send_a, 1)
+        for k in (4, 3, 5, 2, 6, 1, 7):
+            send_a(k)
         recvA[a, t] = sendA[a, t]
 
     got(recvA.at[0, 0:7], rA.at[0])
@@ -162,7 +163,8 @@
         return lax.div(z, 2), 4 * lax.rem(z, 2) + lax.rem(x0 + dx, 4)
 
     def send_stage(delta, a):
-        i, dx = delta + delta // 2, (4 - delta) % 4
+        step = (delta + 3) % 4
+        i, dx = step + step // 2, (4 - delta) % 4
         for dz in FAR:
             pd, pe = device_at(dz, dx)
             src, dst = sendC.at[a, 8 * pd + pe], XG.at[t, a, 8 * i + z0]
@@ -177,14 +179,14 @@
             sendC[a, 8 * dd : 8 * dd + 8] = v[:, cols].reshape(8, 16, 128).astype(BF)
 
     put_slots(0, nn(tx[64:], rx))
-    send_stage(0, 0)
+    send_stage(1, 0)
     got(recvA.at[1, 0:7], rA.at[1])
     ry = recvA[1].astype(F32).reshape(64, 512)
     s0, s1 = (p0 * ry).astype(BF), (p1 * ry).astype(BF)
     put_slots(1, nn(t0[64:], s0) + nn(t1[64:], s1))
-    send_stage(0, 1)
+    send_stage(1, 1)
     for a in range(2):
-        send_stage(1, a)
+        send_stage(2, a)
     xb, gb = nn(tx[:64], rx), nn(t0[:64], s0) + nn(t1[:64], s1)
     for dd in range(4):
         cols = slice(128 * dd, 128 * dd + 128)
@@ -196,7 +198,7 @@
 
     loop(31, send_l)
     pltpu.make_async_copy(sendR.at[b], recvR.at[b], rL).start()
-    for delta in (2, 3):
+    for delta in (3, 0):
         for a in range(2):
             send_stage(delta, a)
 
@@ -371,18 +373,18 @@
         @pl.when(i != 2)
         def _():
             zs[i] = tot.reshape(8, 16, 128).astype(BF)
-            x = lax.rem(x0 + i - lax.div(i, 3), 4)
+            x = lax.rem(x0 + i - lax.div(i, 3) + 1, 4)
             for dz in FAR:
                 z = lax.rem(z0 + dz, 8)
                 pd, pe = lax.div(z, 2), 4 * lax.rem(z, 2) + x
                 if dz:
                     remote(zs.at[i, z], recvZ.at[b], sZ, rZ, (pd, pe, t)).start()
                 else:
-                    @pl.when(i != 0)
+                    @pl.when(i != 4)
                     def _():
                         remote(zs.at[i, z], recvZ.at[b], sZ, rZ, (pd, pe, t)).start()
 
-                    @pl.when(i == 0)
+                    @pl.when(i == 4)
                     def _():
                         pltpu.make_async_copy(zs.at[i, z], recvZ.at[b], rZ).start()
 
@@ -429,7 +431,7 @@
 
         @pl.when(i == S - 3)
         def _():
-            for n in (0, 1):
+            for n in range(3):
                 for m in (0, 1):
                     hid_send(n, m)
 
@@ -453,8 +455,6 @@
     back(S - 2)
     model_grad(1, gg_out)
     back(S - 1)
-    for m in (0, 1):
-        hid_send(2, m)
     hid_relay(0)
     hid_relay(1)
     hid_relay(2)
@@ -472,7 +472,8 @@
         q = lax.rem(t + k, 8)
         remote(sendY.at[q], recvY.at[t], sY, rY, at_t(q)).start()
 
-    loop(8, y_send, 1)
+    for k in (4, 3, 5, 2, 6, 1, 7):
+        y_send(k)
     recvY[t] = sendY[t]
     model_grad(2, gu_out)
     for n in (0, 1):

time: 152 us -> 151 us (level)
  Pallas kernels: 152 us -> 150 us
where the time goes in v7:
time: 151 us
  Pallas kernels  150 us (99%)
    pallas_call x1, Pallas kernels, shards(): pl.pallas_call(kernel, name='expert_back', out_shape=(jax.ShapeDtypeStruc...  148 us

profile of v7, /device:TPU:1, one launch (start us, length us, event | category | flops | bytes accessed | tf_op | source)
XLA Modules:
  0.0 150.9 jit_solution(1476369378106347043)
XLA Ops:
  0.6 147.8 %expert_back.1 = (bf16[8,4096]{1,0:T(8,128)(2,1)S(1)}, bf16[1,1024,896]{2,1,0:T(8,128)(2,1)S(1)}, bf16[1,1024,896]{2,1,0:T(8,128)(2,1)S(1)}, f32[896,1024]{1,0:T...) custom-call(bf16[8,4096]{1,0:T(8,128)(2,1)} %tok_hbm.1, bf16[8,4096]{1,0:T(8,128)(2,1)} %og_hbm.1, ...), custom_call_target="tpu_custom_call" | custom-call | tf_op jit(solution)/shard_map/expert_back/pallas_call | solution.py:524
  148.4 2.5 %put_out.1 = (bf16[8,4096]{1,0:T(8,128)(2,1)}, bf16[1,1024,896]{2,1,0:T(8,128)(2,1)}, bf16[1,1024,896]{2,1,0:T(8,128)(2,1)}, bf16[1,896,1024]{2,1,0:T(8,128)(2,1)}) custom-call(bf16[8,4096]{1,0:T(8,128)(2,1)S(1)} %get-tuple-element.10.yv, bf16[1,1024,896]{2,1,0:T(8,128)(2,1)S(1)} %get-tuple-element.11.gg, bf16[1,1024,896]{2,1,0:T(8,128)(2,1)S(1)} %get-tuple-element.12.gu, ...), custom_call_target="tpu_custom_call" | custom-call | tf_op jit(solution)/shard_map/put_out/pallas_call | solution.py:558
